TPU v7x, 32 devices: a whole 2x2x4 slice. The times are simulated.
32 devices in a mesh: rep: 4 (over z), px: 4 (over x, core), py: 2 (over y).
Axes of the slice: x: 2, y: 2, z: 4, core: 2. Of those that a mesh axis runs over, the one named last changes fastest.
Arguments:
- state: float32 [12, 2, 192, 96, 256], P('rep', None, 'px', 'py'), parts along dimension 0, may hold values from -6 to 6
- cotangent: float32 [12, 2, 192, 96, 256], P('rep', None, 'px', 'py'), parts along dimension 0, may hold values from -6 to 6
- w_in: bfloat16 [512, 192], replicated, may hold values from -0.4375 to 0.4375
- b_in: float32 [512], replicated, may hold values from -5 to 5
- w_out: bfloat16 [192, 512], replicated, may hold values from -0.25 to 0.25
Outputs:
- state_grad: float32 [12, 2, 192, 96, 256], P('rep', None, 'px', 'py'), parts along dimension 0
- grad_in: float32 [512, 768], P(('px', 'py'), 'rep'), parts along dimension 1
- grad_out: float32 [768, 512], P('rep', ('px', 'py')), parts along dimension 0
- grad_bias: float32 [4, 512], P('rep', ('px', 'py')), parts along dimension 0
There are 4 independent parts, one for each index of `rep`. A program takes and returns all parts, laid end to end along the dimension named above; an argument that names none is the same for every part. Nothing has to cross between parts.
All inputs are finite; a program needn't handle non-finite values.
Results may differ from a plain program's by a relative error of at most 0.0065.
The roundings to bfloat16 on the way count: a program that leaves them out, or rounds other values in their place, can miss the bound.
Values may be sent and summed in bfloat16 or wider, within the bound.
No kernel may reach another device: no remote copies, remote signals or barrier semaphores. Data moves between devices by JAX's collectives and lax.ppermute only.
A program may use at most 448 MiB of HBM per device.

v0:
```python
import math

import jax
import jax.numpy as jnp
from jax import lax
from jax.sharding import PartitionSpec as P

PATCH = 4


NU_DT = 5e-05
TIME_STEP = 0.01
FORCING = 20.0


def angles(leading, trailing, length):
    product = leading[:, None] * trailing[None, :] % length
    phases = product.astype(jnp.float32) * (2.0 * math.pi / length)
    factor = 1.0 / math.sqrt(length)
    return (jnp.cos(phases) * factor, jnp.sin(phases) * factor)


def mode_ids(count, length):
    counter = jnp.arange(count, dtype=jnp.int32)
    return jnp.where(counter < count // 2, counter, counter + length - count)


def mode_table(modes, length, direction):
    cosine, sine_part = angles(modes, jnp.arange(length, dtype=jnp.int32), length)
    top_rows = jnp.stack([cosine, direction * sine_part], axis=1)
    low_rows = jnp.stack([-direction * sine_part, cosine], axis=1)
    return jnp.stack([top_rows, low_rows], axis=0).astype(jnp.bfloat16)


def complex_table(length, direction):
    return mode_table(jnp.arange(length, dtype=jnp.int32), length, direction)


def real_table(length, mode_count):
    cosine, sine_part = angles(
        jnp.arange(mode_count, dtype=jnp.int32), jnp.arange(length, dtype=jnp.int32), length
    )
    return jnp.stack([cosine, -sine_part], axis=0).astype(jnp.bfloat16)


def box_order(length, span):
    counter = jnp.arange(length, dtype=jnp.int32)
    local = counter % span
    rows = span // PATCH
    return counter - local + local % rows * PATCH + local // rows


def signed(counter, length):
    return jnp.where(counter < length // 2, counter, counter - length).astype(jnp.float32)


def factors(ky_ids, kz_ids, length, ky_count):
    cutoff = length // 3
    wave_y = signed(ky_ids, ky_count)[:, None, None]
    wave_z = kz_ids.astype(jnp.float32)[None, :, None]
    wave_x = signed(jnp.arange(length, dtype=jnp.int32), length)[None, None, :]
    retained = (
        (jnp.abs(wave_x) <= cutoff) & (jnp.abs(wave_y) <= cutoff) & (wave_z <= cutoff)
    ).astype(jnp.float32)
    square = wave_x * wave_x + wave_y * wave_y + wave_z * wave_z
    damping = jnp.exp(-NU_DT * square)
    weight = jnp.where(kz_ids[None, :, None] == 0, 1.0, 2.0).astype(jnp.float32)
    return ((wave_x, wave_y, wave_z), retained, damping, weight, square)


def cross(former, latter):
    return [
        former[1] * latter[2] - former[2] * latter[1],
        former[2] * latter[0] - former[0] * latter[2],
        former[0] * latter[1] - former[1] * latter[0],
    ]


def curl_modes(waves, spectra):
    real_part = cross(waves, [spectra[slot, 0] for slot in range(3)])
    imag_part = cross(waves, [spectra[slot, 1] for slot in range(3)])
    return jnp.stack([jnp.stack([-imag_part[slot], real_part[slot]]) for slot in range(3)])


def project(waves, square, spectra):
    dotted = waves[0] * spectra[0] + waves[1] * spectra[1] + waves[2] * spectra[2]
    along_k = dotted / jnp.maximum(square, 1.0)
    return jnp.stack([spectra[slot] - waves[slot] * along_k for slot in range(3)])


def to_physical(spectra):
    channels, paired, width_y, width_z, length = spectra.shape
    parts_x = lax.axis_size("px")
    parts_y = lax.axis_size("py")
    order_y = box_order(length, length)
    order_z = box_order(length, length)
    inverse = complex_table(length, 1.0)
    y_table = mode_table(mode_ids(width_y * parts_x, length), length, 1.0)[..., order_y].reshape(
        2, parts_x, width_y, 2, length
    )
    z_table = real_table(length, width_z * parts_y)[..., order_z].reshape(
        2, parts_y, width_z, length
    )
    flat = spectra.astype(jnp.bfloat16).reshape(channels, paired, width_y * width_z, length)
    along_x = jnp.einsum(
        "crpn,rnsx->csxp", flat, inverse, preferred_element_type=jnp.float32
    ).astype(jnp.bfloat16)
    along_x = along_x.reshape(channels, 2, length, 1, width_y * width_z)
    moved = lax.all_to_all(along_x, ("px", "py"), split_axis=2, concat_axis=3, tiled=True)
    blocks = moved.reshape(moved.shape[0], 2, moved.shape[2], parts_x, parts_y, width_y, width_z)
    along_y = jnp.einsum(
        "csxjlam,sjaty->cxtlmy", blocks, y_table, preferred_element_type=jnp.float32
    ).astype(jnp.bfloat16)
    return jnp.einsum(
        "cxtlmy,tlmz->cxyz", along_y, z_table, preferred_element_type=jnp.float32
    ).astype(jnp.bfloat16)


def to_spectral(field, ky_count, mode_count):
    channels, span_x, span_y, length = field.shape
    parts_x = lax.axis_size("px")
    parts_y = lax.axis_size("py")
    width_y = ky_count // parts_x
    width_z = mode_count // parts_y
    order_y = box_order(length, span_y)
    order_z = box_order(length, length)
    forward = complex_table(length, -1.0)
    y_table = (
        mode_table(mode_ids(ky_count, length), length, -1.0)
        .transpose(0, 3, 2, 1)[:, order_y]
        .reshape(2, length, 2, parts_x, width_y)
    )
    z_table = real_table(length, mode_count)[..., order_z].reshape(2, parts_y, width_z, length)
    along_z = jnp.einsum(
        "cxyz,rlmz->crlmxy", field, z_table, preferred_element_type=jnp.float32
    ).astype(jnp.bfloat16)
    along_y = jnp.einsum(
        "crlmxy,rysja->csxjlam", along_z, y_table, preferred_element_type=jnp.float32
    ).astype(jnp.bfloat16)
    along_y = along_y.reshape(channels, 2, span_x, parts_x * parts_y, width_y * width_z)
    moved = lax.all_to_all(along_y, ("px", "py"), split_axis=3, concat_axis=2, tiled=True)
    number = moved.shape[0]
    flat = moved.reshape(number, 2, length, -1)
    along_x = jnp.einsum("csxp,sxtn->ctpn", flat, forward, preferred_element_type=jnp.float32)
    return along_x.reshape(number, 2, width_y, width_z, length)


def to_boxes(field):
    channels, span_x, span_y, span_z = field.shape
    tiles = field.reshape(
        channels, span_x // PATCH, PATCH, PATCH, span_y // PATCH, PATCH, span_z // PATCH
    )
    return tiles.transpose(0, 2, 3, 5, 1, 4, 6).reshape(channels * PATCH**3, -1)


def from_boxes(box_values, layout):
    channels, span_x, span_y, span_z = layout
    tiles = box_values.reshape(
        channels, PATCH, PATCH, PATCH, span_x // PATCH, span_y // PATCH, span_z // PATCH
    )
    return tiles.transpose(0, 4, 1, 2, 5, 3, 6).reshape(layout)


def closure_terms(velocity, force_adj, w_in, b_in, w_out):
    features = to_boxes(velocity)
    adjoints = to_boxes(force_adj)
    pre_act = jnp.dot(w_in, features, preferred_element_type=jnp.float32) + b_in[:, None]
    hidden = jax.nn.silu(pre_act).astype(jnp.bfloat16)
    sigmoid = jax.nn.sigmoid(pre_act)
    hidden_adj = FORCING * jnp.dot(w_out.T, adjoints, preferred_element_type=jnp.float32)
    pre_adj = (hidden_adj * sigmoid * (1.0 + pre_act * (1.0 - sigmoid))).astype(jnp.bfloat16)
    grad_in = jnp.dot(pre_adj, features.T, preferred_element_type=jnp.float32)
    grad_out = FORCING * jnp.dot(adjoints, hidden.T, preferred_element_type=jnp.float32)
    grad_bias = jnp.sum(pre_adj.astype(jnp.float32), axis=1)[None, :]
    feat_adj = jnp.dot(w_in.T, pre_adj, preferred_element_type=jnp.float32)
    return (from_boxes(feat_adj, velocity.shape), grad_in, grad_out, grad_bias)


def pointwise(feat_adj, velocity, vorticity, force_adj):
    vel_list = [velocity[slot].astype(jnp.float32) for slot in range(3)]
    vort_list = [vorticity[slot].astype(jnp.float32) for slot in range(3)]
    force_list = [force_adj[slot].astype(jnp.float32) for slot in range(3)]
    turned = cross(vort_list, force_list)
    vel_adj = jnp.stack([feat_adj[slot] + turned[slot] for slot in range(3)]).astype(jnp.bfloat16)
    vort_adj = jnp.stack(cross(force_list, vel_list)).astype(jnp.bfloat16)
    return (vel_adj, vort_adj)


def shards(state, cotangent, w_in, b_in, w_out):
    width_y = state.shape[2]
    width_z = state.shape[3]
    length = state.shape[4]
    ky_count = width_y * lax.axis_size("px")
    ky_ids = lax.axis_index("px") * width_y + jnp.arange(width_y, dtype=jnp.int32)
    kz_ids = lax.axis_index("py") * width_z + jnp.arange(width_z, dtype=jnp.int32)
    waves, retained, damping, weight, square = factors(ky_ids, kz_ids, length, ky_count)
    kept = retained * state
    spectra = weight * jnp.concatenate([kept, curl_modes(waves, kept)], axis=0)
    force_spec = TIME_STEP * retained * project(waves, square, damping * cotangent)
    fields = to_physical(spectra)
    velocity, vorticity = (fields[:3], fields[3:])
    force_adj = to_physical(force_spec)
    feat_adj, grad_in, grad_out, grad_bias = closure_terms(velocity, force_adj, w_in, b_in, w_out)
    vel_adj, vort_adj = pointwise(feat_adj, velocity, vorticity, force_adj)
    spectral = to_spectral(
        jnp.concatenate([vel_adj, vort_adj], axis=0), ky_count, width_z * lax.axis_size("py")
    )
    state_grad = damping * cotangent + weight * retained * (
        spectral[:3] + curl_modes(waves, spectral[3:])
    )
    grad_in, grad_out, grad_bias = (
        lax.psum_scatter(grad_in, ("px", "py"), scatter_dimension=0, tiled=True),
        lax.psum_scatter(grad_out, ("px", "py"), scatter_dimension=1, tiled=True),
        lax.psum_scatter(grad_bias, ("px", "py"), scatter_dimension=1, tiled=True),
    )
    return (state_grad, grad_in, grad_out, grad_bias)


def solution(mesh):
    return jax.shard_map(
        shards,
        mesh=mesh,
        in_specs=(
            P("rep", None, "px", "py", None),
            P("rep", None, "px", "py", None),
            P(),
            P(),
            P(),
        ),
        out_specs=(
            P("rep", None, "px", "py", None),
            P(("px", "py"), "rep"),
            P("rep", ("px", "py")),
            P("rep", ("px", "py")),
        ),
        check_vma=False,
    )
```

profile of v0, /device:TPU:0, one launch (start us, length us, event | category | flops | bytes accessed | tf_op | source)
XLA Modules:
  0.0 1269.2 jit_solution(7051030765421699349)
XLA Ops:
  46.3 23.6 %copy.130 = bf16[3,2,256,1,2304]{4,1,3,0,2:T(2,128)(2,1)} copy(bf16[3,2,256,1,2304]{4,2,0,1,3:T(8,128)(2,1)S(1)} %fusion.58) | data formatting | bytes 14155776 | tf_op jit(solution)/shard_map/reshape | solution.py:108
  123.5 26.6 %copy.136 = bf16[6,2,256,1,2304]{4,1,3,0,2:T(2,128)(2,1)} copy(bf16[6,2,256,1,2304]{4,2,0,1,3:T(8,128)(2,1)} %fusion.25) | data formatting | bytes 28311552 | tf_op jit(solution)/shard_map/reshape | solution.py:108
  181.4 28.9 %reshape.1115 = bf16[3,2,32,4,2,48,48]{6,5,4,3,2,1,0:T(8,128)(2,1)} reshape(bf16[3,2,32,8,1,2304]{5,3,2,1,0,4:T(8,128)(2,1)} %bitcast.337) | data formatting | bytes 14155776 | tf_op jit(solution)/shard_map/reshape | solution.py:110
  226.6 36.2 %reshape.1116 = bf16[3,8,4,4,64,4,64]{6,5,4,3,2,1,0:T(4,128)(2,1)} reshape(bf16[3,32,256,256]{3,2,1,0:T(8,128)(2,1)} %bitcast_convert_fusion.4) | data formatting | bytes 25165824 | tf_op jit(solution)/shard_map/reshape | solution.py:150
  262.8 22.6 %copy.228 = bf16[3,8,4,4,64,4,64]{6,4,1,5,3,2,0:T(8,128)(2,1)} copy(bf16[3,8,4,4,64,4,64]{6,5,4,3,2,1,0:T(4,128)(2,1)} %reshape.1116) | data formatting | bytes 25165824 | tf_op jit(solution)/shard_map/reshape | solution.py:150
  285.4 29.1 %reshape.1117 = bf16[192,32768]{1,0:T(8,128)(2,1)} reshape(bf16[3,4,4,4,8,64,64]{6,5,4,3,2,1,0:T(8,128)(2,1)} %bitcast.326) | data formatting | bytes 25165824 | tf_op jit(solution)/shard_map/reshape | solution.py:153
  327.4 56.1 %reshape.1119 = bf16[6,2,32,4,2,48,48]{6,5,4,3,2,1,0:T(8,128)(2,1)} reshape(bf16[6,2,32,8,1,2304]{5,3,2,1,0,4:T(8,128)(2,1)} %bitcast.329) | data formatting | bytes 28311552 | tf_op jit(solution)/shard_map/reshape | solution.py:110
  383.5 27.9 %bitcast_convert_fusion.1 = bf16[6,32,256,256]{3,2,1,0:T(8,128)(2,1)} fusion(bf16[2,4,48,2,256,1,1,1]{4,2,1,3,0,7,6,5:T(8,128)(2,1)S(1)} %bitcast.350, bf16[2,2,48,256,1,1]{3,2,1,0,5,4:T(8,128)(2,1)S(1)} %bitcast.346, bf16[6,2,32,4,2,48,48]{6,5,4,3,2,1,0:T(8,128)(2,1)} %reshape.1119), kind=kOutput, calls=%fused_computation.16 | convolution fusion | flops 12101615616 | bytes 39813120 | tf_op jit(solution)/shard_map/cxtlmy,tlmz->cxyz/dot_general | solution.py:114
  422.0 36.4 %reshape.1120 = bf16[3,8,4,4,64,4,64]{6,5,4,3,2,1,0:T(4,128)(2,1)} reshape(bf16[3,32,256,256]{3,2,1,0:T(8,128)(2,1)} %slice.156) | data formatting | bytes 25165824 | tf_op jit(solution)/shard_map/reshape | solution.py:150
  458.3 22.6 %copy.227 = bf16[3,8,4,4,64,4,64]{6,4,1,5,3,2,0:T(8,128)(2,1)} copy(bf16[3,8,4,4,64,4,64]{6,5,4,3,2,1,0:T(4,128)(2,1)} %reshape.1120) | data formatting | bytes 25165824 | tf_op jit(solution)/shard_map/reshape | solution.py:150
  481.0 29.1 %reshape.1121 = bf16[192,32768]{1,0:T(8,128)(2,1)} reshape(bf16[3,4,4,4,8,64,64]{6,5,4,3,2,1,0:T(8,128)(2,1)} %bitcast.327) | data formatting | bytes 25165824 | tf_op jit(solution)/shard_map/reshape | solution.py:153
  510.1 27.8 %fusion.135 = f32[32768,512]{1,0:T(8,128)} fusion(bf16[192,32768]{1,0:T(8,128)(2,1)} %reshape.1121, bf16[512,192]{0,1:T(8,128)(2,1)S(1)} %copy-done), kind=kOutput, calls=%fused_computation.239 | convolution fusion | flops 6442450944 | bytes 79888384 | tf_op jit(solution)/shard_map/dot_general | solution.py:167
  537.9 46.2 %convert_reduce_fusion = (f32[512]{0:T(512)S(1)}, bf16[512,32768]{0,1:T(8,128)(2,1)}) fusion(f32[32768,512]{1,0:T(8,128)} %fusion.135, f32[512]{0:T(512)S(1)} %copy-done.31, bf16[192,32768]{1,0:T(8,128)(2,1)} %reshape.1117, bf16[192,512]{1,0:T(8,128)(2,1)S(1)} %copy-done.30), kind=kOutput, calls=%fused_computation.15 | convolution fusion | flops 6660554240 | bytes 113446912 | tf_op jit(solution)/shard_map/dot_general | solution.py:170
  585.0 25.6 %convolution_bitcast_fusion = f32[192,32768]{1,0:T(8,128)} fusion(bf16[512,32768]{0,1:T(8,128)(2,1)} %get-tuple-element.56, bf16[512,192]{0,1:T(8,128)(2,1)S(1)} %copy-done), kind=kOutput, calls=%fused_computation.18 | convolution fusion | flops 6442450944 | bytes 58916864 | tf_op jit(solution)/shard_map/dot_general | solution.py:175
  610.6 36.4 %reshape.1122 = f32[3,4,4,4,8,64,64]{6,5,4,3,2,1,0:T(8,128)} reshape(f32[192,32768]{1,0:T(8,128)} %convolution_bitcast_fusion) | data formatting | bytes 50331648 | tf_op jit(solution)/shard_map/reshape | solution.py:158
  647.0 55.7 %copy.226 = f32[3,4,4,4,8,64,64]{6,3,5,2,1,4,0:T(4,128)} copy(f32[3,4,4,4,8,64,64]{6,5,4,3,2,1,0:T(8,128)} %reshape.1122) | data formatting | bytes 50331648 | tf_op jit(solution)/shard_map/reshape | solution.py:158
  702.7 32.7 %fusion.132 = (f32[1,8,4,4,64,4,64]{6,5,4,3,2,1,0:T(4,128)}, f32[1,8,4,4,64,4,64]{6,5,4,3,2,1,0:T(4,128)}, f32[1,8,4,4,64,4,64]{6,5,4,3,2,1,0:T(4,128)}) fusion(f32[3,8,4,4,64,4,64]{6,5,4,3,2,1,0:T(4,128)} %bitcast.325), kind=kLoop, calls=%fused_computation.236 | loop fusion | bytes 50331648 | tf_op jit(solution)/shard_map/slice | solution.py:184
  834.6 19.8 %fusion.13 = bf16[2,2,48,6,32,256]{5,2,0,4,1,3:T(8,128)(2,1)} fusion(bf16[6,32,256,256]{3,2,1,0:T(8,128)(2,1)} %fusion.61, bf16[2,2,48,256,1,1]{3,2,1,0,5,4:T(8,128)(2,1)S(1)} %bitcast.347), kind=kOutput, calls=%fused_computation.27 | convolution fusion | flops 4831838208 | bytes 44138496 | tf_op jit(solution)/shard_map/cxyz,rlmz->crlmxy/dot_general | solution.py:134
  854.3 50.7 %fusion.7 = bf16[6,2,32,4,2,48,48]{6,5,2,4,0,3,1:T(8,128)(2,1)} fusion(bf16[2,2,48,6,32,256]{5,2,0,4,1,3:T(8,128)(2,1)} %fusion.13, bf16[2,256,2,4,48,1,1,1]{1,4,3,2,0,7,6,5:T(8,128)(2,1)S(1)} %bitcast.348), kind=kOutput, calls=%fused_computation.19 | convolution fusion | flops 7254835200 | bytes 33423360 | tf_op jit(solution)/shard_map/crlmxy,rysja->csxjlam/dot_general | solution.py:137
  905.1 26.0 %copy.189 = bf16[6,2,32,4,2,48,48]{6,5,2,1,0,4,3:T(8,128)(2,1)} copy(bf16[6,2,32,4,2,48,48]{6,5,2,4,0,3,1:T(8,128)(2,1)} %fusion.7) | data formatting | bytes 28311552 | tf_op jit(solution)/shard_map/reshape | solution.py:140
  931.1 51.2 %reshape.1172 = bf16[6,2,32,8,2304]{4,2,1,0,3:T(8,128)(2,1)} reshape(bf16[6,2,32,4,2,48,48]{6,5,2,1,0,4,3:T(8,128)(2,1)} %copy.189) | data formatting | bytes 28311552 | tf_op jit(solution)/shard_map/reshape | solution.py:140
  987.8 18.3 %fusion.136 = f32[512,192]{1,0:T(8,128)} fusion(bf16[512,32768]{0,1:T(8,128)(2,1)} %get-tuple-element.56, bf16[192,32768]{1,0:T(8,128)(2,1)} %reshape.1121), kind=kOutput, calls=%fused_computation.240 | convolution fusion | flops 6442450944 | bytes 46530560 | tf_op jit(solution)/shard_map/dot_general | solution.py:172
  1006.2 31.2 %fusion.78 = f32[192,512]{0,1:T(8,128)} fusion(bf16[192,32768]{1,0:T(8,128)(2,1)} %reshape.1117, f32[32768,512]{1,0:T(8,128)} %fusion.135, f32[512]{0:T(512)S(1)} %copy-done.32), kind=kOutput, calls=%fused_computation.136 | convolution fusion | flops 6543212544 | bytes 80087040 | tf_op jit(solution)/shard_map/dot_general | solution.py:173
  1038.8 108.1 %all-to-all-done.2 = bf16[6,2,32,8,2304]{4,2,1,0,3:T(8,128)(2,1)} async-done(((bf16[6,2,32,8,2304]{4,2,1,0,3:T(8,128)(2,1)}), bf16[6,2,32,8,2304]{4,2,1,0,3:T(8,128)(2,1)}, u32[]{:S(2)}, u32[]{:S(2)}) %all-to-all-start.2) | async-done | bytes 14155808 | tf_op jit(solution)/shard_map/all_to_all | solution.py:141
  (176 shorter events, 385.5 us)
Async XLA Ops:
  7.2 502.9 %copy-start = (bf16[512,192]{0,1:T(8,128)(2,1)S(1)}, bf16[512,192]{0,1:T(8,128)(2,1)}, u32[]{:S(2)}) copy-start(bf16[512,192]{0,1:T(8,128)(2,1)} %param.7) | copy-start | bytes 589828
  8.3 12.5 copy-start.27
  8.8 67.1 %copy-start.19 = (f32[48]{0:T(128)}, f32[48]{0:T(128)S(1)}, u32[]{:S(2)}) copy-start(f32[48]{0:T(128)S(1)} %get-tuple-element.65) | copy-start | bytes 580
  70.0 84.8 %all-to-all-start = ((bf16[3,2,256,1,2304]{4,1,3,0,2:T(2,128)(2,1)}), bf16[3,2,256,1,2304]{4,1,3,0,2:T(2,128)(2,1)}, u32[]{:S(2)}, u32[]{:S(2)}) async-start(bf16[3,2,256,1,2304]{4,1,3,0,2:T(2,128)(2,1)} %copy.130), calls=%async_computation | async-start | bytes 14155776 | tf_op jit(solution)/shard_map/all_to_all | solution.py:109
  154.8 160.5 %all-to-all-start.1 = ((bf16[6,2,256,1,2304]{4,1,3,0,2:T(2,128)(2,1)}), bf16[6,2,256,1,2304]{4,1,3,0,2:T(2,128)(2,1)}, u32[]{:S(2)}, u32[]{:S(2)}) async-start(bf16[6,2,256,1,2304]{4,1,3,0,2:T(2,128)(2,1)} %copy.136), calls=%async_computation.1 | async-start | bytes 28311552 | tf_op jit(solution)/shard_map/all_to_all | solution.py:109
  160.3 877.1 %reduce-scatter.10.cloned.1.call-start = ((), (), s32[]{:S(2)}) async-start(), calls=%async_computation.8 | async-start | bytes 294912
  162.4 221.1 %copy-start.10 = (bf16[2,96,256]{2,1,0:T(8,128)(2,1)}, bf16[2,96,256]{2,1,0:T(8,128)(2,1)S(1)}, u32[]{:S(2)}) copy-start(bf16[2,96,256]{2,1,0:T(8,128)(2,1)S(1)} %copy.126) | copy-start | bytes 294916
  510.1 27.8 %copy-start.30 = (bf16[192,512]{1,0:T(8,128)(2,1)S(1)}, bf16[192,512]{1,0:T(8,128)(2,1)}, u32[]{:S(2)}) copy-start(bf16[192,512]{1,0:T(8,128)(2,1)} %param.9) | copy-start | bytes 589828
  510.1 27.8 %copy-start.31 = (f32[512]{0:T(512)S(1)}, f32[512]{0:T(512)}, u32[]{:S(2)}) copy-start(f32[512]{0:T(512)} %param.8) | copy-start | bytes 6148
  783.0 25.0 %slice-start = ((s8[12582912]{0:T(1024)(128)(4,1)}), s8[4194304]{0:T(1024)(128)(4,1)S(1)}, s32[]{:S(2)}) async-start(s8[12582912]{0:T(1024)(128)(4,1)} %bitcast.323), calls=%async_computation.9 | async-start | bytes 8388608
  783.0 25.0 %slice-start.1 = ((s8[12582912]{0:T(1024)(128)(4,1)}), s8[4194304]{0:T(1024)(128)(4,1)S(1)}, s32[]{:S(2)}) async-start(s8[12582912]{0:T(1024)(128)(4,1)} %bitcast.323), calls=%async_computation.10 | async-start | bytes 8388608
  783.0 25.0 %slice-start.7 = ((s8[8388608]{0:T(1024)(128)(4,1)}), s8[4194304]{0:T(1024)(128)(4,1)S(1)}, s32[]{:S(2)}) async-start(s8[8388608]{0:T(1024)(128)(4,1)} %bitcast.335), calls=%async_computation.16 | async-start | bytes 8388608
  795.3 12.6 slice-start.2
  795.3 12.6 slice-start.8
  834.6 19.8 %copy-start.12 = (bf16[2,256,2,192]{1,3,2,0:T(8,128)(2,1)S(1)}, bf16[2,256,2,192]{1,3,2,0:T(8,128)(2,1)}, u32[]{:S(2)}) copy-start(bf16[2,256,2,192]{1,3,2,0:T(8,128)(2,1)} %copy.124) | copy-start | bytes 1179652
  982.2 164.7 %all-to-all-start.2 = ((bf16[6,2,32,8,2304]{4,2,1,0,3:T(8,128)(2,1)}), bf16[6,2,32,8,2304]{4,2,1,0,3:T(8,128)(2,1)}, u32[]{:S(2)}, u32[]{:S(2)}) async-start(bf16[6,2,32,8,2304]{4,2,1,0,3:T(8,128)(2,1)} %reshape.1172), calls=%async_computation.2 | async-start | bytes 28311552 | tf_op jit(solution)/shard_map/all_to_all | solution.py:141
  987.7 18.4 %copy-start.32 = (f32[512]{0:T(512)S(1)}, f32[512]{0:T(512)}, u32[]{:S(2)}) copy-start(f32[512]{0:T(512)} %param.8) | copy-start | bytes 6148
  987.8 274.4 %reduce-scatter.6.cloned.1.call-start = ((), (), s32[]{:S(2)}) async-start(), calls=%async_computation.6 | async-start | bytes 589824 | tf_op jit(solution)/shard_map/reduce_scatter | solution.py:212
  1006.1 256.0 %reduce-scatter.8.cloned.1.call-start = ((), (), s32[]{:S(2)}) async-start(), calls=%async_computation.7 | async-start | bytes 589824 | tf_op jit(solution)/shard_map/reduce_scatter | solution.py:213
  1146.9 10.6 copy-start.9
  1193.8 15.2 %copy-start.20 = (f32[48]{0:T(128)S(1)}, f32[48]{0:T(128)}, u32[]{:S(2)}) copy-start(f32[48]{0:T(128)} %copy-done.19) | copy-start | bytes 580
  1193.8 15.2 %copy-start.23 = (f32[48]{0:T(128)S(1)}, f32[48]{0:T(128)}, u32[]{:S(2)}) copy-start(f32[48]{0:T(128)} %get-tuple-element.66) | copy-start | bytes 580
  1193.8 15.2 %copy-start.26 = (f32[256]{0:T(256)S(1)}, f32[256]{0:T(256)}, u32[]{:S(2)}) copy-start(f32[256]{0:T(256)} %fusion.120) | copy-start | bytes 3076
  1247.3 14.8 %copy-start.1 = (bf16[512,192]{0,1:T(8,128)(2,1)S(1)}, bf16[512,192]{0,1:T(8,128)(2,1)}, u32[]{:S(2)}) copy-start(bf16[512,192]{0,1:T(8,128)(2,1)} %param.7) | copy-start | bytes 589828
  (24 other events, 162.1 us)
Sparse Core Ops, SparseCore 0:
  585.2 35.3 reduce-scatter.9
  1006.2 38.0 reduce-scatter.5
  1047.9 73.2 reduce-scatter.7
where the time goes:
time: 1290 us; the launch traced here: 1270 us
  local copies, waits for them, and re-layouts  680 us (53%)
  matrix products  307 us (24%)
  other arithmetic  136 us (11%)
  waiting for transfers between devices  114 us (9%)
  starting transfers between devices  17 us (1%)
  between operations  14.8 us (1%)
    reshape x4, local copies, waits for them, and re-layouts, to_boxes(): field.reshape(channels, span_x // PATCH, PATCH, PATCH, span_y // PATCH, P...  118 us
    all_to_all x1, waiting for transfers between devices, to_spectral(): lax.all_to_all(along_y, ('px', 'py'), split_axis=3, concat_axis=2, tiled=...  108 us
    reshape x2, local copies, waits for them, and re-layouts, from_boxes(): box_values.reshape(channels, PATCH, PATCH, PATCH, span_x // PATCH, span_y...  92 us
    reshape x2, local copies, waits for them, and re-layouts, to_physical(): moved.reshape(moved.shape[0], 2, moved.shape[2], parts_x, parts_y, width_...  85.1 us
    reshape x2, local copies, waits for them, and re-layouts, to_spectral(): along_y.reshape(channels, 2, span_x, parts_x * parts_y, width_y * width_z)  77.1 us
    reshape x2, local copies, waits for them, and re-layouts, to_boxes(): tiles.transpose(0, 2, 3, 5, 1, 4, 6).reshape(channels * PATCH ** 3, -1)  58.2 us
    dot_general x1, matrix products, to_spectral(): jnp.einsum('crlmxy,rysja->csxjlam', along_z, y_table, preferred_element_t...  50.7 us
    reshape x2, local copies, waits for them, and re-layouts, to_physical(): along_x = along_x.reshape(channels, 2, length, 1, width_y * width_z)  50.2 us
  transfers between devices with their start and end apart: 6, of which 3 were waited for; matrix products, arithmetic and copies ran while one was open for 62% of the time, Pallas kernels for 0%

commit v1 on v0

v1 whole, which is shorter than its diff:
```python
import functools
import math

import jax
import jax.numpy as jnp
from jax import lax
from jax.experimental import pallas as pl
from jax.experimental.pallas import tpu as pltpu
from jax.sharding import PartitionSpec as P

PATCH = 4
NU_DT = 5e-05
TIME_STEP = 0.01
FORCING = 20.0
LANES = 128
F32 = jnp.float32
BF16 = jnp.bfloat16

OUT_SLOTS = ("uy", "uz", "ux", "wy", "wz", "fx", "fy", "fz")
BACK_SLOTS = ("ax", "az", "gy", "gz", "ay")


def up_to(value, step):
    return -(-value // step) * step


def angles(leading, trailing, length):
    product = leading[:, None] * trailing[None, :] % length
    phases = product.astype(F32) * (2.0 * math.pi / length)
    factor = 1.0 / math.sqrt(length)
    return jnp.cos(phases) * factor, jnp.sin(phases) * factor


def mode_ids(count, length):
    counter = jnp.arange(count, dtype=jnp.int32)
    return jnp.where(counter < count // 2, counter, counter + length - count)


def box_order(length):
    counter = jnp.arange(length, dtype=jnp.int32)
    boxes = length // PATCH
    return counter % boxes * PATCH + counter // boxes


def signed(counter, length):
    return jnp.where(counter < length // 2, counter, counter - length).astype(F32)


def dot(a, b):
    return lax.dot_general(a, b, (((1,), (0,)), ((), ())), preferred_element_type=F32)


def dot_nt(a, b):
    return lax.dot_general(a, b, (((1,), (1,)), ((), ())), preferred_element_type=F32)


def dot_tn(a, b):
    return lax.dot_general(a, b, (((0,), (0,)), ((), ())), preferred_element_type=F32)


def lane_modes(slot, width_z, lanes, first):
    local = jnp.arange(lanes, dtype=jnp.int32) - slot * width_z
    inside = (local >= 0) & (local < width_z)
    return jnp.where(inside, local, 0) + first, inside


def vregs_of(slot, width_z):
    return list(range(slot * width_z // LANES, ((slot + 1) * width_z - 1) // LANES + 1))


def spectra_kernel(ky_ref, kz_ref, state_ref, cot_ref, out_ref, *, block, length):
    cutoff = float(length // 3)
    wave_z = kz_ref[...]
    counter = lax.broadcasted_iota(jnp.int32, wave_z.shape, 1)
    wave_x = jnp.where(counter < length // 2, counter, counter - length).astype(F32)
    plane = wave_x * wave_x + wave_z * wave_z
    inside = (jnp.abs(wave_x) <= cutoff) & (wave_z <= cutoff)
    weight = jnp.where(wave_z == 0.0, 1.0, 2.0).astype(F32)
    base = pl.program_id(0) * block

    def one(k, carry):
        wave_y = ky_ref[base + k]
        kept = jnp.where(inside & (jnp.abs(wave_y) <= cutoff), 1.0, 0.0).astype(F32)
        square = plane + wave_y * wave_y
        damped = jnp.exp(-NU_DT * square)
        scale = kept * weight
        push = kept * damped * TIME_STEP
        inverse = 1.0 / jnp.maximum(square, 1.0)
        u = [[scale * state_ref[c, r, k] for r in range(2)] for c in range(3)]
        for r in range(2):
            lanes = pl.ds(r * length, length)
            g = [push * cot_ref[c, r, k] for c in range(3)]
            along = (wave_x * g[0] + wave_y * g[1] + wave_z * g[2]) * inverse
            sign = -1.0 if r == 0 else 1.0
            q = 1 - r
            wy = sign * (wave_z * u[0][q] - wave_x * u[2][q])
            wz = sign * (wave_x * u[1][q] - wave_y * u[0][q])
            fx = g[0] - wave_x * along
            fy = g[1] - wave_y * along
            fz = g[2] - wave_z * along
            rows = (u[1][r], u[2][r], u[0][r], wy, wz, fx, fy, fz)
            for slot, value in enumerate(rows):
                out_ref[k, slot, :, lanes] = value.astype(BF16)
        return carry

    lax.fori_loop(0, block, one, 0)


def make_spectra(ky, kz_col, state, cotangent):
    _, _, width_y, width_z, length = state.shape
    block = 8
    slots = len(OUT_SLOTS)
    spec = pl.BlockSpec((3, 2, block, width_z, length), lambda i: (0, 0, i, 0, 0))
    return pl.pallas_call(
        functools.partial(spectra_kernel, block=block, length=length),
        grid=(width_y // block,),
        in_specs=[
            pl.BlockSpec(memory_space=pltpu.SMEM),
            pl.BlockSpec((width_z, length), lambda i: (0, 0)),
            spec,
            spec,
        ],
        out_specs=pl.BlockSpec((block, slots, width_z, 2 * length), lambda i: (i, 0, 0, 0)),
        out_shape=jax.ShapeDtypeStruct((width_y, slots, width_z, 2 * length), BF16),
        compiler_params=pltpu.CompilerParams(vmem_limit_bytes=56 * 2**20),
        name="spectra",
    )(ky, kz_col, state, cotangent)


def along_x_kernel(table_ref, spec_ref, out_ref, scratch, *, block, rows, width_y, span):
    step = pl.program_id(0)
    lanes = out_ref.shape[3]
    table = table_ref[...]
    live = spec_ref.shape[1]

    def one(k, carry):
        value = dot_nt(table, spec_ref[k])
        start = pl.multiple_of((step * block + k) * rows, 8)
        for v in range(lanes // LANES):
            if (v + 1) * LANES <= live:
                piece = value[:, v * LANES : (v + 1) * LANES]
                scratch[v, pl.ds(start, rows), :] = piece
            else:
                scratch[v, pl.ds(start, rows), :] = jnp.zeros((rows, LANES), F32)
                scratch[v, pl.ds(start, rows), pl.ds(0, live - v * LANES)] = value[:, v * LANES :]
        return carry

    lax.fori_loop(0, block, one, 0)

    @pl.when(step == pl.num_programs(0) - 1)
    def _():
        def move(i, carry):
            dest = i // span
            x = i % span
            for v in range(lanes // LANES):
                parts = [scratch[v, pl.ds(2 * i + s, width_y, stride=rows), :] for s in range(2)]
                block_rows = jnp.concatenate(parts, axis=0).astype(BF16)
                out_ref[dest, x, :, pl.ds(v * LANES, LANES)] = block_rows
            return carry

        lax.fori_loop(0, rows // 2, move, 0)


def along_x(table, spectra, parts, span):
    width_y, live, depth = spectra.shape
    rows = table.shape[0]
    block = 8
    lanes = up_to(live, LANES)
    shape = (parts, span, 2 * width_y, lanes)
    return pl.pallas_call(
        functools.partial(along_x_kernel, block=block, rows=rows, width_y=width_y, span=span),
        grid=(width_y // block,),
        in_specs=[
            pl.BlockSpec((rows, depth), lambda i: (0, 0)),
            pl.BlockSpec((block, live, depth), lambda i: (i, 0, 0)),
        ],
        out_specs=pl.BlockSpec(shape, lambda i: (0, 0, 0, 0)),
        out_shape=jax.ShapeDtypeStruct(shape, BF16),
        scratch_shapes=[pltpu.VMEM((lanes // LANES, width_y * rows, LANES), F32)],
        compiler_params=pltpu.CompilerParams(vmem_limit_bytes=56 * 2**20),
        cost_estimate=pl.CostEstimate(
            flops=2 * rows * live * depth * width_y * 2,
            bytes_accessed=2 * (width_y * live * depth + rows * width_y * lanes),
            transcendentals=0,
        ),
        name="along_x",
    )(table, spectra)


def halves(low, high):
    left = lax.broadcasted_iota(jnp.int32, low.shape, 1) < LANES // 2
    turned_high = pltpu.roll(high, LANES // 2, 1)
    turned_low = pltpu.roll(low, LANES // 2, 1)
    return jnp.where(left, low, turned_high), jnp.where(left, turned_low, high)


def physical_kernel(
    recv_ref,
    ky_ref,
    kz_in_ref,
    kz_back_ref,
    ty_ref,
    tyb_ref,
    w_in_ref,
    w_in_t_ref,
    w_out_t_ref,
    bias_ref,
    *refs,
    parts_x,
    parts_y,
    width_y,
    width_z,
    length,
    back_lanes,
):
    z_refs = dict(zip(("uy", "uz", "ux", "wy", "wz", "fx", "fy", "fz", "wx"), refs[:9]))
    zb_ref = refs[9]
    out_ref, gin_ref, gout_ref = refs[10:13]
    mid, vel, force, vort, fadj, back = refs[13:]
    rows = 2 * width_y
    in_lanes = recv_ref.shape[3]
    boxes = length // PATCH
    feats = 3 * PATCH * PATCH

    @pl.when(pl.program_id(0) == 0)
    def _():
        gin_ref[...] = jnp.zeros(gin_ref.shape, F32)
        gout_ref[...] = jnp.zeros(gout_ref.shape, F32)

    def section_y(dx, carry):
        for py in range(parts_y):
            whole = jnp.concatenate(
                [recv_ref[px * parts_y + py, dx] for px in range(parts_x)], axis=0
            )
            first = whole[:, :LANES].astype(F32)
            second = pltpu.roll(first, LANES - width_z, 1)
            mixed = ky_ref[...] * second - kz_in_ref[py : py + 1, :] * first
            turned = []
            for px in range(parts_x):
                turned.append(-mixed[px * rows + width_y : (px + 1) * rows])
                turned.append(mixed[px * rows : px * rows + width_y])
            extra = jnp.concatenate(turned, axis=0).astype(BF16)
            mid[py, dx, :, pl.ds(0, in_lanes)] = dot(ty_ref[...], whole).astype(BF16)
            mid[py, dx, :, pl.ds(in_lanes, LANES)] = dot(ty_ref[...], extra).astype(BF16)
        return carry

    lax.fori_loop(0, PATCH, section_y, 0)

    def section_z(dx, carry):
        def field(name):
            if name == "wx":
                vregs = [in_lanes // LANES]
            else:
                vregs = vregs_of(OUT_SLOTS.index(name), width_z)
            pieces = [
                mid[py, dx, pl.ds(t * length, length), pl.ds(v * LANES, LANES)]
                for py in range(parts_y)
                for t in range(2)
                for v in vregs
            ]
            return dot(jnp.concatenate(pieces, axis=1), z_refs[name][...])

        for slot, name in enumerate("xyz"):
            at = pl.multiple_of((slot * PATCH + dx) * length, length)
            rows_here = pl.ds(at, length)
            for target, kind in ((vel, "u"), (force, "f")):
                value = field(kind + name).astype(BF16).astype(F32)
                for half in range(length // LANES):
                    target[half, rows_here, :] = value[:, half * LANES : (half + 1) * LANES]
            vort[rows_here, :] = field("w" + name).astype(BF16)
        return carry

    lax.fori_loop(0, PATCH, section_z, 0)

    pair = 2

    def gather(source, by):
        per_dz = []
        for half in range(2):
            got = [source[half, pl.ds(by + i, feats, stride=boxes), :] for i in range(2 * pair)]
            one = halves(got[0], got[1])
            two = halves(got[2], got[3])
            per_dz.append(jnp.concatenate([one[0], two[0]], axis=1))
            per_dz.append(jnp.concatenate([one[1], two[1]], axis=1))
        return jnp.concatenate(per_dz, axis=0).astype(BF16)

    def closure(step, carry):
        by = step * 2 * pair
        features = gather(vel, by)
        adjoints = gather(force, by)
        pre = dot(w_in_ref[...], features) + bias_ref[...]
        sigma = 0.5 * jnp.tanh(0.5 * pre) + 0.5
        hidden = (pre * sigma).astype(BF16)
        hidden_adj = FORCING * dot(w_out_t_ref[...], adjoints)
        pre_adj = (hidden_adj * sigma * (1.0 + pre * (1.0 - sigma))).astype(BF16)
        ones = jnp.ones((gin_ref.shape[1] - features.shape[0], features.shape[1]), BF16)
        gin_ref[...] += dot_nt(pre_adj, jnp.concatenate([features, ones], axis=0))
        gout_ref[...] += dot_nt(hidden, adjoints)
        back_feat = dot(w_in_t_ref[...], pre_adj)
        for half in range(2):
            low = back_feat[(2 * half) * feats : (2 * half + 1) * feats]
            high = back_feat[(2 * half + 1) * feats : (2 * half + 2) * feats]
            for p in range(2):
                cut = slice(p * LANES, (p + 1) * LANES)
                for i, value in enumerate(halves(low[:, cut], high[:, cut])):
                    fadj[half, pl.ds(by + 2 * p + i, feats, stride=boxes), :] = value
        return carry

    lax.fori_loop(0, boxes // (2 * pair), closure, 0)

    back_vregs = back_lanes // LANES

    def section_back(dx, carry):
        def rows_at(slot):
            return pl.ds(pl.multiple_of((slot * PATCH + dx) * length, length), length)

        def read(source, slot):
            return jnp.concatenate(
                [source[half, rows_at(slot), :] for half in range(length // LANES)], axis=1
            )

        u = [read(vel, c) for c in range(3)]
        f = [read(force, c) for c in range(3)]
        w = [vort[rows_at(c), :].astype(F32) for c in range(3)]
        named = {}
        for c, name in enumerate("xyz"):
            a, b = (c + 1) % 3, (c + 2) % 3
            turned = read(fadj, c) + (w[a] * f[b] - w[b] * f[a])
            named["v" + name] = turned.astype(BF16)
            named["g" + name] = (f[a] * u[b] - f[b] * u[a]).astype(BF16)
        at = 0
        for group, names in enumerate(back_groups(width_z)):
            joined = jnp.concatenate([named[name] for name in names], axis=1)
            depth = joined.shape[1]
            for py in range(parts_y):
                value = dot(joined, zb_ref[py, pl.ds(at, depth), :]).astype(BF16)
                for r in range(2):
                    piece = value[:, r * LANES : (r + 1) * LANES]
                    back[py, pl.ds(r * length, length), pl.ds(group * LANES, LANES)] = piece
            at += depth
        for py in range(parts_y):
            value = dot(tyb_ref[...], back[py])
            by_y = ky_ref[...] * value[:, back_lanes : back_lanes + LANES]
            by_z = value[:, back_lanes + LANES :]
            extra = []
            for v in range(back_vregs):
                here = kz_back_ref[py, v : v + 1, :] * by_z
                if v == 0:
                    here = here + by_y
                extra.append(here)
            extra = jnp.concatenate(extra, axis=1)
            for px in range(parts_x):
                re = slice(px * rows, px * rows + width_y)
                im = slice(px * rows + width_y, (px + 1) * rows)
                total = jnp.concatenate(
                    [value[re, :back_lanes] - extra[im], value[im, :back_lanes] + extra[re]], axis=0
                )
                out_ref[px * parts_y + py, dx] = total.astype(BF16)
        return carry

    lax.fori_loop(0, PATCH, section_back, 0)


def back_groups(width_z):
    names = [{"a": "v", "g": "g"}[slot[0]] + slot[1] for slot in BACK_SLOTS]
    lanes = up_to(len(BACK_SLOTS) * width_z, LANES)
    groups = []
    for v in range(lanes // LANES):
        groups.append([n for slot, n in enumerate(names) if v in vregs_of(slot, width_z)])
    groups.append(["gz", "gx"])
    groups.append(["gy", "gx"])
    return groups


def back_table(width_z, length, parts_y):
    names = [{"a": "v", "g": "g"}[slot[0]] + slot[1] for slot in BACK_SLOTS]
    lanes = up_to(len(BACK_SLOTS) * width_z, LANES)
    groups = back_groups(width_z)
    order = box_order(length)

    def piece(slot, vreg, py, sign):
        modes, inside = lane_modes(slot, width_z, lanes, py * width_z)
        cut = slice(vreg * LANES, (vreg + 1) * LANES)
        cosine, sine = angles(order, modes[cut], length)
        keep = sign * inside[cut].astype(F32)[None, :]
        return jnp.concatenate([cosine * keep, -sine * keep], axis=1)

    ky_slots = {"gz": (BACK_SLOTS.index("ax"), 1.0), "gx": (BACK_SLOTS.index("az"), -1.0)}
    kz_slots = {"gy": (BACK_SLOTS.index("ax"), -1.0), "gx": (BACK_SLOTS.index("ay"), 1.0)}
    tables = []
    for py in range(parts_y):
        rows = []
        for v, group in enumerate(groups[:-2]):
            rows += [piece(names.index(n), v, py, 1.0) for n in group]
        for which, group in ((ky_slots, groups[-2]), (kz_slots, groups[-1])):
            for n in group:
                slot, sign = which[n]
                rows.append(sum(piece(slot, v, py, sign) for v in vregs_of(slot, width_z)))
        tables.append(jnp.concatenate(rows, axis=0))
    return jnp.stack(tables).astype(BF16)


def out_table(slot, width_z, length, parts_y):
    lanes = (vregs_of(slot, width_z)[-1] + 1) * LANES
    order = box_order(length)
    rows = []
    for py in range(parts_y):
        modes, inside = lane_modes(slot, width_z, lanes, py * width_z)
        cosine, sine = angles(modes, order, length)
        keep = inside.astype(F32)[:, None]
        for value in (cosine, -sine):
            for v in vregs_of(slot, width_z):
                rows.append((value * keep)[v * LANES : (v + 1) * LANES])
    return jnp.concatenate(rows, axis=0).astype(BF16)


def physical(recv, ky_rows, kz_in, kz_back, tables, weights, grid_sizes, back_lanes):
    parts_x, parts_y, width_y, width_z, length = grid_sizes
    parts, span, rows, in_lanes = recv.shape
    hid = weights[0].shape[0]
    feat = weights[0].shape[1]
    t_y, t_yb, z_tables, z_back = tables

    def whole(array):
        return pl.BlockSpec(array.shape, lambda i: (0,) * array.ndim)

    small = [ky_rows, kz_in, kz_back, t_y, t_yb, *weights, *z_tables, z_back]
    feat_pad = up_to(feat + 1, 2 * LANES)
    field = (3 * PATCH * length, length)
    split = (length // LANES, 3 * PATCH * length, LANES)
    flops = 2 * span * parts_y * (2 * length) * (parts_x * rows) * (in_lanes + LANES)
    flops += 2 * 5 * hid * feat * (span * length * length // PATCH**3)
    flops += 2 * span * length * length * length * (9 * 2 + 20)
    return pl.pallas_call(
        functools.partial(
            physical_kernel,
            parts_x=parts_x,
            parts_y=parts_y,
            width_y=width_y,
            width_z=width_z,
            length=length,
            back_lanes=back_lanes,
        ),
        grid=(span // PATCH,),
        in_specs=[pl.BlockSpec((parts, PATCH, rows, in_lanes), lambda i: (0, i, 0, 0))]
        + [whole(a) for a in small],
        out_specs=[
            pl.BlockSpec((parts, PATCH, rows, back_lanes), lambda i: (0, i, 0, 0)),
            pl.BlockSpec((hid, feat_pad), lambda i: (0, 0)),
            pl.BlockSpec((hid, feat), lambda i: (0, 0)),
        ],
        out_shape=[
            jax.ShapeDtypeStruct((parts, span, rows, back_lanes), BF16),
            jax.ShapeDtypeStruct((hid, feat_pad), F32),
            jax.ShapeDtypeStruct((hid, feat), F32),
        ],
        scratch_shapes=[
            pltpu.VMEM((parts_y, PATCH, 2 * length, in_lanes + LANES), BF16),
            pltpu.VMEM(split, F32),
            pltpu.VMEM(split, F32),
            pltpu.VMEM(field, BF16),
            pltpu.VMEM(split, F32),
            pltpu.VMEM((parts_y, 2 * length, back_lanes + 2 * LANES), BF16),
        ],
        compiler_params=pltpu.CompilerParams(vmem_limit_bytes=58 * 2**20),
        cost_estimate=pl.CostEstimate(
            flops=flops, bytes_accessed=2 * recv.size * 2, transcendentals=0
        ),
        name="physical",
    )(recv, *small)


def final_kernel(
    ky_ref, kz_ref, table_ref, cot_ref, *refs, steps_in, block, chunks, span, parts, width_y, width_z, length
):
    recv_refs = refs[:chunks]
    out_ref, scratch, turned = refs[chunks:]
    step = pl.program_id(0)
    rows = 2 * width_y
    lanes = recv_refs[0].shape[3]

    @pl.when(step < steps_in)
    def _():
        for j in range(chunks):
            def load(x, carry):
                at = ((step * chunks + j) * span + x) * rows
                value = recv_refs[j][0, x].astype(F32)
                for v in range(lanes // LANES):
                    cut = value[:, v * LANES : (v + 1) * LANES]
                    scratch[v, pl.ds(pl.multiple_of(at, 8), rows), :] = cut
                return carry

            lax.fori_loop(0, span, load, 0)

    @pl.when(step >= steps_in)
    def _():
        cutoff = float(length // 3)
        wave_z = kz_ref[...]
        counter = lax.broadcasted_iota(jnp.int32, wave_z.shape, 1)
        wave_x = jnp.where(counter < length // 2, counter, counter - length).astype(F32)
        plane = wave_x * wave_x + wave_z * wave_z
        inside = (jnp.abs(wave_x) <= cutoff) & (wave_z <= cutoff)
        weight = jnp.where(wave_z == 0.0, 1.0, 2.0).astype(F32)

        def one(k, carry):
            ky = (step - steps_in) * block + k
            pieces = []
            for v in range(lanes // LANES):
                parts_s = [
                    scratch[v, pl.ds(ky + s * width_y, length, stride=rows), :] for s in range(2)
                ]
                pieces.append(jnp.concatenate(parts_s, axis=0))
            gathered = jnp.concatenate(pieces, axis=1).astype(BF16)
            turned[...] = dot_tn(gathered, table_ref[...])
            wave_y = ky_ref[ky]
            kept = jnp.where(inside & (jnp.abs(wave_y) <= cutoff), 1.0, 0.0).astype(F32)
            damped = jnp.exp(-NU_DT * (plane + wave_y * wave_y))
            scale = kept * weight

            def part(name, t):
                at = BACK_SLOTS.index(name) * width_z
                return turned[pl.ds(at, width_z), pl.ds(t * length, length)]

            for t in range(2):
                sign = -1.0 if t == 0 else 1.0
                ax = part("ax", t)
                ay = part("ay", t) - sign * wave_x * part("gz", 1 - t)
                az = part("az", t) + sign * wave_x * part("gy", 1 - t)
                for c, value in enumerate((ax, ay, az)):
                    out_ref[c, t, k] = damped * cot_ref[c, t, k] + scale * value
            return carry

        lax.fori_loop(0, block, one, 0)


def finish(ky, kz_col, table, cotangent, received):
    _, _, width_y, width_z, length = cotangent.shape
    parts, span, rows, lanes = received[0].shape
    chunks = len(received)
    block = 8
    steps_in = parts
    steps = steps_in + width_y // block
    spec = pl.BlockSpec(
        (3, 2, block, width_z, length), lambda i: (0, 0, jnp.maximum(i - steps_in, 0), 0, 0)
    )
    recv_spec = pl.BlockSpec(
        (1, span, rows, lanes), lambda i: (jnp.minimum(i, steps_in - 1), 0, 0, 0)
    )
    return pl.pallas_call(
        functools.partial(
            final_kernel,
            steps_in=steps_in,
            block=block,
            chunks=chunks,
            span=span,
            parts=parts,
            width_y=width_y,
            width_z=width_z,
            length=length,
        ),
        grid=(steps,),
        in_specs=[
            pl.BlockSpec(memory_space=pltpu.SMEM),
            pl.BlockSpec((width_z, length), lambda i: (0, 0)),
            pl.BlockSpec(table.shape, lambda i: (0, 0)),
            spec,
        ]
        + [recv_spec] * chunks,
        out_specs=spec,
        out_shape=jax.ShapeDtypeStruct(cotangent.shape, F32),
        scratch_shapes=[
            pltpu.VMEM((lanes // LANES, length * rows, LANES), F32),
            pltpu.VMEM((lanes, 2 * length), F32),
        ],
        compiler_params=pltpu.CompilerParams(vmem_limit_bytes=60 * 2**20),
        name="finish",
    )(ky, kz_col, table, cotangent, *received)


def shards(state, cotangent, w_in, b_in, w_out):
    width_y, width_z, length = state.shape[2:]
    parts_x = lax.axis_size("px")
    parts_y = lax.axis_size("py")
    parts = parts_x * parts_y
    slab = length // parts
    chunks = 4
    while chunks > 1 and slab % (chunks * PATCH) != 0:
        chunks //= 2
    span = slab // chunks
    ky_count = width_y * parts_x
    hid, feat = w_in.shape

    ky_ids = lax.axis_index("px") * width_y + jnp.arange(width_y, dtype=jnp.int32)
    kz_ids = lax.axis_index("py") * width_z + jnp.arange(width_z, dtype=jnp.int32)
    ky = signed(ky_ids, ky_count)
    kz_col = jnp.broadcast_to(kz_ids.astype(F32)[:, None], (width_z, length))

    everything = jnp.arange(length, dtype=jnp.int32)
    cosine, sine = angles(everything, everything, length)
    x_rows = jnp.stack(
        [jnp.concatenate([cosine, -sine], axis=1), jnp.concatenate([sine, cosine], axis=1)], axis=1
    ).astype(BF16)
    x_rows = x_rows.reshape(parts, chunks, span, 2, 2 * length)

    order = box_order(length)
    cosine_y, sine_y = angles(order, mode_ids(ky_count, length), length)
    cosine_y = cosine_y.reshape(length, parts_x, 1, width_y)
    sine_y = sine_y.reshape(length, parts_x, 1, width_y)
    t_y = jnp.concatenate(
        [
            jnp.concatenate([cosine_y, -sine_y], axis=2).reshape(length, -1),
            jnp.concatenate([sine_y, cosine_y], axis=2).reshape(length, -1),
        ],
        axis=0,
    ).astype(BF16)
    t_yb = t_y.T

    z_tables = [out_table(slot, width_z, length, parts_y) for slot in range(len(OUT_SLOTS))]
    z_tables.append(out_table(0, width_z, length, parts_y))
    z_back = back_table(width_z, length, parts_y)

    back_lanes = up_to(len(BACK_SLOTS) * width_z, LANES)
    ky_all = signed(jnp.arange(ky_count, dtype=jnp.int32), ky_count).reshape(parts_x, 1, width_y)
    ky_rows = jnp.broadcast_to(ky_all, (parts_x, 2, width_y)).reshape(-1, 1)
    ky_rows = jnp.broadcast_to(ky_rows, (2 * ky_count, LANES))
    kz_in, kz_back = [], []
    for py in range(parts_y):
        modes, inside = lane_modes(0, width_z, LANES, py * width_z)
        kz_in.append(jnp.where(inside, modes, 0))
        total = jnp.zeros((back_lanes,), jnp.int32)
        for name in ("ax", "ay"):
            modes, inside = lane_modes(BACK_SLOTS.index(name), width_z, back_lanes, py * width_z)
            total = total + jnp.where(inside, modes, 0)
        kz_back.append(total.reshape(-1, LANES))
    kz_in = jnp.stack(kz_in).astype(F32)
    kz_back = jnp.stack(kz_back).astype(F32)

    def turn(weight):
        split = weight.reshape(hid, 3, PATCH, PATCH, PATCH)
        return split.transpose(0, 4, 1, 2, 3).reshape(hid, feat)

    w_in_f = turn(w_in)
    w_out_t = turn(w_out.T)
    bias = jnp.broadcast_to(b_in[:, None], (hid, 2 * LANES))
    weights = (w_in_f, w_in_f.T, w_out_t, bias)

    spectra = make_spectra(ky, kz_col, state, cotangent)
    spectra = spectra.reshape(width_y, -1, 2 * length)
    exchange = functools.partial(
        lax.all_to_all, axis_name=("px", "py"), split_axis=0, concat_axis=0, tiled=True
    )
    arrived = []
    for j in range(chunks):
        table = x_rows[:, j].reshape(parts * span * 2, 2 * length)
        arrived.append(exchange(along_x(table, spectra, parts, span)))
    grid_sizes = (parts_x, parts_y, width_y, width_z, length)
    tables = (t_y, t_yb, z_tables, z_back)
    returned = []
    grads = 0.0
    for recv in arrived:
        sent, gin, gout = physical(
            recv, ky_rows, kz_in, kz_back, tables, weights, grid_sizes, back_lanes
        )
        returned.append(exchange(sent))
        grads = grads + jnp.concatenate([gin, gout], axis=1)

    x_back = jnp.concatenate(
        [
            jnp.concatenate([cosine, -sine], axis=1),
            jnp.concatenate([sine, cosine], axis=1),
        ],
        axis=0,
    ).astype(BF16)
    state_grad = finish(ky, kz_col, x_back, cotangent, returned)

    grads = exchange(grads.reshape(parts, hid // parts, -1))
    grads = jnp.sum(grads, axis=0)
    own = hid // parts
    pad = up_to(feat + 1, 2 * LANES)

    def unturn(weight):
        split = weight.reshape(own, PATCH, 3, PATCH, PATCH)
        return split.transpose(0, 2, 3, 4, 1).reshape(own, feat)

    grad_in = unturn(grads[:, :feat])
    grad_bias = grads[:, feat][None, :]
    grad_out = FORCING * unturn(grads[:, pad:]).T
    return state_grad, grad_in, grad_out, grad_bias


def solution(mesh):
    return jax.shard_map(
        shards,
        mesh=mesh,
        in_specs=(
            P("rep", None, "px", "py", None),
            P("rep", None, "px", "py", None),
            P(),
            P(),
            P(),
        ),
        out_specs=(
            P("rep", None, "px", "py", None),
            P(("px", "py"), "rep"),
            P("rep", ("px", "py")),
            P("rep", ("px", "py")),
        ),
        check_vma=False,
    )
```

time: 1290 us -> 728 us (0.56)
  local copies, waits for them, and re-layouts: 680 us -> 19.1 us
  Pallas kernels: 0 us -> 423 us
  matrix products: 307 us -> 0 us
  blocking collectives: 0 us -> 139 us
  other arithmetic: 136 us -> 45.8 us
  waiting for transfers between devices: 114 us -> 67 us
    reshape x14 -> x8, local copies, waits for them, and re-layouts: 480 us -> 2.07 us  [the longest x4 1.8 us: turn(): return split.transpose(0, 4, 1, 2, 3).reshape(hid, feat)]
    pallas_call x0 -> x10, Pallas kernels: none -> 423 us  [the longest x4 257 us: physical(): pl.pallas_call(functools.partial(physical_kernel, parts_x=parts_x, parts_...]
    dot_general x12 -> x0, matrix products: 307 us -> none  [the longest x1 50.7 us: to_spectral(): jnp.einsum('crlmxy,rysja->csxjlam', along_z, y_table, preferred_element_t...]
    all_to_all x0 -> x4, blocking collectives: none -> 139 us  [the longest x3 121 us: shards(): returned.append(exchange(sent))]
    slice x6 -> x29, local copies, waits for them, and re-layouts: 101 us -> 6.75 us  [the longest x10 5.47 us: out_table(): rows.append((value * keep)[v * LANES:(v + 1) * LANES])]
    squeeze x3 -> x0, local copies, waits for them, and re-layouts: 47.6 us -> none  [pointwise(): feat_adj[slot] + turned[slot]]
    all_to_all x3 -> x5, waiting for transfers between devices: 114 us -> 67 us  [the longest x4 36.8 us: shards(): arrived.append(exchange(along_x(table, spectra, parts, span)))]
    unnamed x8 -> x18, other arithmetic: 45 us -> 0.31 us
  transfers between devices with their start and end apart: 6 -> 5, of which waited for: 3 -> 4; matrix products, arithmetic and copies ran while one was open for 62% -> 8% of each run, Pallas kernels for 0% -> 37%
where the time goes in v1:
time: 728 us; the launch traced here: 720 us
  Pallas kernels  423 us (58%)
  blocking collectives  139 us (19%)
  waiting for transfers between devices  67 us (9%)
  other arithmetic  45.8 us (6%)
  starting transfers between devices  23.2 us (3%)
  local copies, waits for them, and re-layouts  19.1 us (3%)
    pallas_call x4, Pallas kernels, physical(): pl.pallas_call(functools.partial(physical_kernel, parts_x=parts_x, parts_...  257 us
    all_to_all x3, blocking collectives, shards(): returned.append(exchange(sent))  121 us
    pallas_call x4, Pallas kernels, along_x(): pl.pallas_call(functools.partial(along_x_kernel, block=block, rows=rows,...  98.9 us
    pallas_call x1, Pallas kernels, finish(): pl.pallas_call(functools.partial(final_kernel, steps_in=steps_in, block=b...  48.9 us
    all_to_all x4, waiting for transfers between devices, shards(): arrived.append(exchange(along_x(table, spectra, parts, span)))  36.8 us
    all_to_all x1, waiting for transfers between devices, shards(): returned.append(exchange(sent))  30.2 us
    all_to_all x4, starting transfers between devices, shards(): arrived.append(exchange(along_x(table, spectra, parts, span)))  19.6 us
    another operation x10, other arithmetic  18.8 us
  transfers between devices with their start and end apart: 5, of which 4 were waited for; matrix products, arithmetic and copies ran while one was open for 8% of the time, Pallas kernels for 37%

profile of v1, /device:TPU:0, one launch (start us, length us, event | category | flops | bytes accessed | tf_op | source)
XLA Modules:
  0.0 719.7 jit_solution(1008453294879094619)
XLA Ops:
  4.1 18.0 %spectra.1 = bf16[48,8,48,512]{3,2,1,0:T(8,128)(2,1)} custom-call(f32[48]{0:T(128)} %fusion.138.ky_ref, f32[48,256]{1,0:T(8,128)} %broadcast_in_dim.81.kz_ref, f32[3,2,48,48,256]{4,3,2,1,0:T(8,128)} %state_ref.1, f32[3,2,48,48,256]{4,3,2,1,0:T(8,128)} %cot_ref.3), custom_call_target="tpu_custom_call" | custom-call | tf_op jit(solution)/shard_map/spectra/pallas_call | solution.py:114
  22.1 24.7 %along_x.7 = bf16[8,8,96,384]{3,2,1,0:T(8,128)(2,1)} custom-call(bf16[128,512]{1,0:T(8,128)(2,1)} %reshape_squeeze.15.table_ref, bf16[48,384,512]{2,1,0:T(8,128)(2,1)} %bitcast.50), custom_call_target="tpu_custom_call" | custom-call | flops 4831838208 | bytes 23592960 | tf_op jit(solution)/shard_map/along_x/pallas_call | solution.py:170
  46.8 5.2 all-to-all-start.6
  65.4 24.8 %along_x.6 = bf16[8,8,96,384]{3,2,1,0:T(8,128)(2,1)} custom-call(bf16[128,512]{1,0:T(8,128)(2,1)} %reshape_squeeze.14.table_ref, bf16[48,384,512]{2,1,0:T(8,128)(2,1)} %bitcast.51), custom_call_target="tpu_custom_call" | custom-call | flops 4831838208 | bytes 23592960 | tf_op jit(solution)/shard_map/along_x/pallas_call | solution.py:170
  90.1 15.8 %all-to-all-done.6.recv_ref = bf16[8,8,96,384]{3,2,1,0:T(8,128)(2,1)} async-done(((bf16[8,8,96,384]{3,2,1,0:T(8,128)(2,1)}), bf16[8,8,96,384]{3,2,1,0:T(8,128)(2,1)}, u32[]{:S(2)}, u32[]{:S(2)}) %all-to-all-start.6) | async-done | bytes 4718624 | tf_op jit(solution)/shard_map/all_to_all | solution.py:655
  106.0 4.7 all-to-all-start.4
  121.7 4.6 multiply_convert_fusion.24
  127.9 24.8 %along_x.5 = bf16[8,8,96,384]{3,2,1,0:T(8,128)(2,1)} custom-call(bf16[128,512]{1,0:T(8,128)(2,1)} %reshape_squeeze.13.table_ref, bf16[48,384,512]{2,1,0:T(8,128)(2,1)} %bitcast.52), custom_call_target="tpu_custom_call" | custom-call | flops 4831838208 | bytes 23592960 | tf_op jit(solution)/shard_map/along_x/pallas_call | solution.py:170
  152.7 11.8 %all-to-all-done.4.recv_ref = bf16[8,8,96,384]{3,2,1,0:T(8,128)(2,1)} async-done(((bf16[8,8,96,384]{3,2,1,0:T(8,128)(2,1)}), bf16[8,8,96,384]{3,2,1,0:T(8,128)(2,1)}, u32[]{:S(2)}, u32[]{:S(2)}) %all-to-all-start.4) | async-done | bytes 4718624 | tf_op jit(solution)/shard_map/all_to_all | solution.py:655
  164.5 4.8 all-to-all-start.2
  189.4 24.7 %along_x.4 = bf16[8,8,96,384]{3,2,1,0:T(8,128)(2,1)} custom-call(bf16[128,512]{1,0:T(8,128)(2,1)} %reshape_squeeze.12.table_ref, bf16[48,384,512]{2,1,0:T(8,128)(2,1)} %bitcast.53), custom_call_target="tpu_custom_call" | custom-call | flops 4831838208 | bytes 23592960 | tf_op jit(solution)/shard_map/along_x/pallas_call | solution.py:170
  214.1 9.1 %all-to-all-done.2.recv_ref = bf16[8,8,96,384]{3,2,1,0:T(8,128)(2,1)} async-done(((bf16[8,8,96,384]{3,2,1,0:T(8,128)(2,1)}), bf16[8,8,96,384]{3,2,1,0:T(8,128)(2,1)}, u32[]{:S(2)}, u32[]{:S(2)}) %all-to-all-start.2) | async-done | bytes 4718624 | tf_op jit(solution)/shard_map/all_to_all | solution.py:655
  223.2 4.8 all-to-all-start
  229.8 64.2 %physical.7 = (bf16[8,8,96,256]{3,2,1,0:T(8,128)(2,1)}, f32[512,256]{1,0:T(8,128)}, f32[512,192]{1,0:T(8,128)}) custom-call(bf16[8,8,96,384]{3,2,1,0:T(8,128)(2,1)} %all-to-all-done.6.recv_ref, f32[384,128]{1,0:T(8,128)} %broadcast_in_dim.84.ky_ref, f32[2,128]{1,0:T(2,128)} %add_convert_fusion.1.kz_in_ref, f32[2,2,128]{2,1,0:T(2,128)} %add_convert_fusion.kz_back_ref, ...), custom_call_target="tpu_custom_call" | custom-call | flops 21474836480 | bytes 9437184 | tf_op jit(solution)/shard_map/physical/pallas_call | solution.py:434
  294.0 64.1 %physical.6 = (bf16[8,8,96,256]{3,2,1,0:T(8,128)(2,1)}, f32[512,256]{1,0:T(8,128)}, f32[512,192]{1,0:T(8,128)}) custom-call(bf16[8,8,96,384]{3,2,1,0:T(8,128)(2,1)} %all-to-all-done.4.recv_ref, f32[384,128]{1,0:T(8,128)} %broadcast_in_dim.84.ky_ref, f32[2,128]{1,0:T(2,128)} %add_convert_fusion.1.kz_in_ref, f32[2,2,128]{2,1,0:T(2,128)} %add_convert_fusion.kz_back_ref, ...), custom_call_target="tpu_custom_call" | custom-call | flops 21474836480 | bytes 9437184 | tf_op jit(solution)/shard_map/physical/pallas_call | solution.py:434
  358.2 64.1 %physical.5 = (bf16[8,8,96,256]{3,2,1,0:T(8,128)(2,1)}, f32[512,256]{1,0:T(8,128)}, f32[512,192]{1,0:T(8,128)}) custom-call(bf16[8,8,96,384]{3,2,1,0:T(8,128)(2,1)} %all-to-all-done.2.recv_ref, f32[384,128]{1,0:T(8,128)} %broadcast_in_dim.84.ky_ref, f32[2,128]{1,0:T(2,128)} %add_convert_fusion.1.kz_in_ref, f32[2,2,128]{2,1,0:T(2,128)} %add_convert_fusion.kz_back_ref, ...), custom_call_target="tpu_custom_call" | custom-call | flops 21474836480 | bytes 9437184 | tf_op jit(solution)/shard_map/physical/pallas_call | solution.py:434
  422.4 64.6 %physical.4 = (bf16[8,8,96,256]{3,2,1,0:T(8,128)(2,1)}, f32[512,256]{1,0:T(8,128)}, f32[512,192]{1,0:T(8,128)}) custom-call(bf16[8,8,96,384]{3,2,1,0:T(8,128)(2,1)} %all-to-all-done.recv_ref, f32[384,128]{1,0:T(8,128)} %broadcast_in_dim.84.ky_ref, f32[2,128]{1,0:T(2,128)} %add_convert_fusion.1.kz_in_ref, f32[2,2,128]{2,1,0:T(2,128)} %add_convert_fusion.kz_back_ref, ...), custom_call_target="tpu_custom_call" | custom-call | flops 21474836480 | bytes 9437184 | tf_op jit(solution)/shard_map/physical/pallas_call | solution.py:434
  488.7 18.5 %all_to_all.45 = f32[8,64,448]{2,1,0:T(8,128)} all-to-all(f32[8,64,448]{2,1,0:T(8,128)S(1)} %fusion.1), channel_id=1, replica_groups=mesh['rep'=4,'px'=4,'py'=2] {'px','py'}, dimensions={0} | all-to-all | bytes 1835008 | tf_op jit(solution)/shard_map/all_to_all | solution.py:676
  507.2 40.4 %all_to_all.46.refs_3_ = bf16[8,8,96,256]{3,2,1,0:T(8,128)(2,1)} all-to-all(bf16[8,8,96,256]{3,2,1,0:T(8,128)(2,1)S(1)} %copy-done.1), channel_id=1, replica_groups=mesh['rep'=4,'px'=4,'py'=2] {'px','py'}, dimensions={0} | all-to-all | bytes 6291456 | tf_op jit(solution)/shard_map/all_to_all | solution.py:664
  547.5 40.4 %all_to_all.47.refs_2_ = bf16[8,8,96,256]{3,2,1,0:T(8,128)(2,1)} all-to-all(bf16[8,8,96,256]{3,2,1,0:T(8,128)(2,1)S(1)} %copy-done.2), channel_id=1, replica_groups=mesh['rep'=4,'px'=4,'py'=2] {'px','py'}, dimensions={0} | all-to-all | bytes 6291456 | tf_op jit(solution)/shard_map/all_to_all | solution.py:664
  587.9 40.1 %all_to_all.48.refs_1_ = bf16[8,8,96,256]{3,2,1,0:T(8,128)(2,1)} all-to-all(bf16[8,8,96,256]{3,2,1,0:T(8,128)(2,1)S(1)} %copy-done.3), channel_id=1, replica_groups=mesh['rep'=4,'px'=4,'py'=2] {'px','py'}, dimensions={0} | all-to-all | bytes 6291456 | tf_op jit(solution)/shard_map/all_to_all | solution.py:664
  628.0 3.7 all-to-all-start.1
  638.4 30.2 %all-to-all-done.1.refs_0_ = bf16[8,8,96,256]{3,2,1,0:T(8,128)(2,1)S(1)} async-done(((bf16[8,8,96,256]{3,2,1,0:T(8,128)(2,1)}), bf16[8,8,96,256]{3,2,1,0:T(8,128)(2,1)S(1)}, u32[]{:S(2)}, u32[]{:S(2)}) %all-to-all-start.1) | async-done | bytes 3145760 | tf_op jit(solution)/shard_map/all_to_all | solution.py:664
  670.4 48.9 %finish.1 = f32[3,2,48,48,256]{4,3,2,1,0:T(8,128)} custom-call(f32[48]{0:T(128)} %fusion.138.ky_ref, f32[48,256]{1,0:T(8,128)} %broadcast_in_dim.81.kz_ref, bf16[512,512]{1,0:T(8,128)(2,1)} %maximum_maximum_fusion.table_ref, f32[3,2,48,48,256]{4,3,2,1,0:T(8,128)} %cot_ref.3, bf16[8,8,96,256]{3,2,1,0:T(8,128)(2,1)} %copy-done, ...), custom_call_target="tpu_custom_call" | custom-call | tf_op jit(solution)/shard_map/finish/pallas_call | solution.py:549
  (261 shorter events, 60.3 us)
Async XLA Ops:
  46.8 59.2 %all-to-all-start.6 = ((bf16[8,8,96,384]{3,2,1,0:T(8,128)(2,1)}), bf16[8,8,96,384]{3,2,1,0:T(8,128)(2,1)}, u32[]{:S(2)}, u32[]{:S(2)}) async-start(bf16[8,8,96,384]{3,2,1,0:T(8,128)(2,1)} %along_x.7), calls=%async_computation.6 | async-start | bytes 9437184 | tf_op jit(solution)/shard_map/all_to_all | solution.py:655
  52.1 69.6 %copy-start.17 = (s32[256]{0:T(256)}, s32[256]{0:T(256)S(1)}, u32[]{:S(2)}) copy-start(s32[256]{0:T(256)S(1)} %fusion.133) | copy-start | bytes 3076
  52.1 69.6 %copy-start.19 = (s32[256]{0:T(256)}, s32[256]{0:T(256)S(1)}, u32[]{:S(2)}) copy-start(s32[256]{0:T(256)S(1)} %broadcast_add_fusion.7) | copy-start | bytes 3076
  52.1 59.1 %copy-start.34 = (s32[256]{0:T(256)}, s32[256]{0:T(256)S(1)}, u32[]{:S(2)}) copy-start(s32[256]{0:T(256)S(1)} %fusion.127) | copy-start | bytes 3076
  52.2 59.1 %copy-start.35 = (s32[256]{0:T(256)}, s32[256]{0:T(256)S(1)}, u32[]{:S(2)}) copy-start(s32[256]{0:T(256)S(1)} %broadcast_add_fusion.3) | copy-start | bytes 3076
  52.2 8.4 %copy-start.24 = (s32[256]{0:T(256)}, s32[256]{0:T(256)S(1)}, u32[]{:S(2)}) copy-start(s32[256]{0:T(256)S(1)} %fusion.131) | copy-start | bytes 3076
  52.2 8.4 %copy-start.26 = (s32[256]{0:T(256)}, s32[256]{0:T(256)S(1)}, u32[]{:S(2)}) copy-start(s32[256]{0:T(256)S(1)} %broadcast_add_fusion.5) | copy-start | bytes 3076
  52.2 59.0 %copy-start.28 = (s32[256]{0:T(256)}, s32[256]{0:T(256)S(1)}, u32[]{:S(2)}) copy-start(s32[256]{0:T(256)S(1)} %fusion.132) | copy-start | bytes 3076
  52.3 59.0 %copy-start.30 = (s32[256]{0:T(256)}, s32[256]{0:T(256)S(1)}, u32[]{:S(2)}) copy-start(s32[256]{0:T(256)S(1)} %broadcast_add_fusion.6) | copy-start | bytes 3076
  90.1 27.6 %copy-start.11 = (bf16[512,192]{0,1:T(8,128)(2,1)S(1)}, bf16[512,192]{0,1:T(8,128)(2,1)}, u32[]{:S(2)}) copy-start(bf16[512,192]{0,1:T(8,128)(2,1)} %param.7) | copy-start | bytes 589828
  106.0 58.5 %all-to-all-start.4 = ((bf16[8,8,96,384]{3,2,1,0:T(8,128)(2,1)}), bf16[8,8,96,384]{3,2,1,0:T(8,128)(2,1)}, u32[]{:S(2)}, u32[]{:S(2)}) async-start(bf16[8,8,96,384]{3,2,1,0:T(8,128)(2,1)} %along_x.6), calls=%async_computation.4 | async-start | bytes 9437184 | tf_op jit(solution)/shard_map/all_to_all | solution.py:655
  164.5 58.7 %all-to-all-start.2 = ((bf16[8,8,96,384]{3,2,1,0:T(8,128)(2,1)}), bf16[8,8,96,384]{3,2,1,0:T(8,128)(2,1)}, u32[]{:S(2)}, u32[]{:S(2)}) async-start(bf16[8,8,96,384]{3,2,1,0:T(8,128)(2,1)} %along_x.5), calls=%async_computation.2 | async-start | bytes 9437184 | tf_op jit(solution)/shard_map/all_to_all | solution.py:655
  214.1 14.0 %copy-start.23 = (f32[512]{0:T(512)S(1)}, f32[512]{0:T(512)}, u32[]{:S(2)}) copy-start(f32[512]{0:T(512)} %param.8) | copy-start | bytes 6148
  223.2 199.2 %all-to-all-start = ((bf16[8,8,96,384]{3,2,1,0:T(8,128)(2,1)}), bf16[8,8,96,384]{3,2,1,0:T(8,128)(2,1)}, u32[]{:S(2)}, u32[]{:S(2)}) async-start(bf16[8,8,96,384]{3,2,1,0:T(8,128)(2,1)} %along_x.4), calls=%async_computation | async-start | bytes 9437184 | tf_op jit(solution)/shard_map/all_to_all | solution.py:655
  422.3 64.7 %copy-start.5 = (f32[512,256]{1,0:T(8,128)S(1)}, f32[512,256]{1,0:T(8,128)}, u32[]{:S(2)}) copy-start(f32[512,256]{1,0:T(8,128)} %get-tuple-element.26) | copy-start | bytes 1572868
  422.3 64.7 %copy-start.6 = (f32[512,192]{1,0:T(8,128)S(1)}, f32[512,192]{1,0:T(8,128)}, u32[]{:S(2)}) copy-start(f32[512,192]{1,0:T(8,128)} %get-tuple-element.27) | copy-start | bytes 1179652
  422.3 64.7 %copy-start.7 = (f32[512,256]{1,0:T(8,128)S(1)}, f32[512,256]{1,0:T(8,128)}, u32[]{:S(2)}) copy-start(f32[512,256]{1,0:T(8,128)} %get-tuple-element.24) | copy-start | bytes 1572868
  422.3 64.7 %copy-start.8 = (f32[512,192]{1,0:T(8,128)S(1)}, f32[512,192]{1,0:T(8,128)}, u32[]{:S(2)}) copy-start(f32[512,192]{1,0:T(8,128)} %get-tuple-element.25) | copy-start | bytes 1179652
  422.3 64.7 %copy-start.9 = (f32[512,256]{1,0:T(8,128)S(1)}, f32[512,256]{1,0:T(8,128)}, u32[]{:S(2)}) copy-start(f32[512,256]{1,0:T(8,128)} %get-tuple-element.22) | copy-start | bytes 1572868
  422.4 64.7 %copy-start.10 = (f32[512,192]{1,0:T(8,128)S(1)}, f32[512,192]{1,0:T(8,128)}, u32[]{:S(2)}) copy-start(f32[512,192]{1,0:T(8,128)} %get-tuple-element.23) | copy-start | bytes 1179652
  487.0 20.2 %copy-start.1 = (bf16[8,8,96,256]{3,2,1,0:T(8,128)(2,1)S(1)}, bf16[8,8,96,256]{3,2,1,0:T(8,128)(2,1)}, u32[]{:S(2)}) copy-start(bf16[8,8,96,256]{3,2,1,0:T(8,128)(2,1)} %get-tuple-element.19) | copy-start | bytes 9437188
  507.2 40.4 %copy-start.2 = (bf16[8,8,96,256]{3,2,1,0:T(8,128)(2,1)S(1)}, bf16[8,8,96,256]{3,2,1,0:T(8,128)(2,1)}, u32[]{:S(2)}) copy-start(bf16[8,8,96,256]{3,2,1,0:T(8,128)(2,1)} %get-tuple-element.18) | copy-start | bytes 9437188
  547.5 40.4 %copy-start.3 = (bf16[8,8,96,256]{3,2,1,0:T(8,128)(2,1)S(1)}, bf16[8,8,96,256]{3,2,1,0:T(8,128)(2,1)}, u32[]{:S(2)}) copy-start(bf16[8,8,96,256]{3,2,1,0:T(8,128)(2,1)} %get-tuple-element.17) | copy-start | bytes 9437188
  628.0 40.6 %all-to-all-start.1 = ((bf16[8,8,96,256]{3,2,1,0:T(8,128)(2,1)}), bf16[8,8,96,256]{3,2,1,0:T(8,128)(2,1)S(1)}, u32[]{:S(2)}, u32[]{:S(2)}) async-start(bf16[8,8,96,256]{3,2,1,0:T(8,128)(2,1)} %get-tuple-element.16), calls=%async_computation.1 | async-start | bytes 6291456 | tf_op jit(solution)/shard_map/all_to_all | solution.py:664
  (34 other events, 91.4 us)

commit v2 on v1

v2 whole, which is shorter than its diff:
```python
import functools
import math

import jax
import jax.numpy as jnp
import numpy as np
from jax import lax
from jax.experimental import pallas as pl
from jax.experimental.pallas import tpu as pltpu
from jax.sharding import PartitionSpec as P


PATCH = 4
NU_DT = 5e-05
TIME_STEP = 0.01
FORCING = 20.0
LANES = 128
F32 = jnp.float32
BF16 = jnp.bfloat16

OUT_SLOTS = ("uy", "uz", "ux", "wy", "wz", "fx", "fy", "fz")
MAX_CHUNKS = 4
PAIRS = 2
HID_BLOCKS = 1
UNROLL = 4
BACK_SLOTS = ("ax", "az", "gy", "gz", "ay")


def up_to(value, step):
    return -(-value // step) * step


def angles(leading, trailing, length):
    product = np.asarray(leading)[:, None] * np.asarray(trailing)[None, :] % length
    phases = product.astype(np.float32) * np.float32(2.0 * math.pi / length)
    factor = np.float32(1.0 / math.sqrt(length))
    return np.cos(phases) * factor, np.sin(phases) * factor


def mode_ids(count, length):
    counter = np.arange(count)
    return np.where(counter < count // 2, counter, counter + length - count)


def box_order(length):
    counter = np.arange(length)
    boxes = length // PATCH
    return counter % boxes * PATCH + counter // boxes


def signed(counter, length):
    return jnp.where(counter < length // 2, counter, counter - length).astype(F32)


def dot(a, b):
    return lax.dot_general(a, b, (((1,), (0,)), ((), ())), preferred_element_type=F32)


def dot_nt(a, b):
    return lax.dot_general(a, b, (((1,), (1,)), ((), ())), preferred_element_type=F32)


def dot_tn(a, b):
    return lax.dot_general(a, b, (((0,), (0,)), ((), ())), preferred_element_type=F32)


def lane_modes(slot, width_z, lanes, first):
    local = np.arange(lanes) - slot * width_z
    inside = (local >= 0) & (local < width_z)
    return np.where(inside, local, 0) + first, inside


def vregs_of(slot, width_z):
    return list(range(slot * width_z // LANES, ((slot + 1) * width_z - 1) // LANES + 1))


def spectra_kernel(ky_ref, kz_ref, state_ref, cot_ref, out_ref, *, block, length):
    cutoff = float(length // 3)
    wave_z = kz_ref[...]
    counter = lax.broadcasted_iota(jnp.int32, wave_z.shape, 1)
    wave_x = jnp.where(counter < length // 2, counter, counter - length).astype(F32)
    plane = wave_x * wave_x + wave_z * wave_z
    inside = (jnp.abs(wave_x) <= cutoff) & (wave_z <= cutoff)
    weight = jnp.where(wave_z == 0.0, 1.0, 2.0).astype(F32)
    base = pl.program_id(0) * block

    def one(k, carry):
        wave_y = ky_ref[base + k]
        kept = jnp.where(inside & (jnp.abs(wave_y) <= cutoff), 1.0, 0.0).astype(F32)
        square = plane + wave_y * wave_y
        damped = jnp.exp(-NU_DT * square)
        scale = kept * weight
        push = kept * damped * TIME_STEP
        inverse = 1.0 / jnp.maximum(square, 1.0)
        u = [[scale * state_ref[c, r, k] for r in range(2)] for c in range(3)]
        for r in range(2):
            lanes = pl.ds(r * length, length)
            g = [push * cot_ref[c, r, k] for c in range(3)]
            along = (wave_x * g[0] + wave_y * g[1] + wave_z * g[2]) * inverse
            sign = -1.0 if r == 0 else 1.0
            q = 1 - r
            wy = sign * (wave_z * u[0][q] - wave_x * u[2][q])
            wz = sign * (wave_x * u[1][q] - wave_y * u[0][q])
            fx = g[0] - wave_x * along
            fy = g[1] - wave_y * along
            fz = g[2] - wave_z * along
            rows = (u[1][r], u[2][r], u[0][r], wy, wz, fx, fy, fz)
            for slot, value in enumerate(rows):
                out_ref[k, slot, :, lanes] = value.astype(BF16)
        return carry

    lax.fori_loop(0, block, one, 0)


def make_spectra(ky, kz_col, state, cotangent):
    _, _, width_y, width_z, length = state.shape
    block = 8
    slots = len(OUT_SLOTS)
    spec = pl.BlockSpec((3, 2, block, width_z, length), lambda i: (0, 0, i, 0, 0))
    return pl.pallas_call(
        functools.partial(spectra_kernel, block=block, length=length),
        grid=(width_y // block,),
        in_specs=[
            pl.BlockSpec(memory_space=pltpu.SMEM),
            pl.BlockSpec((width_z, length), lambda i: (0, 0)),
            spec,
            spec,
        ],
        out_specs=pl.BlockSpec((block, slots, width_z, 2 * length), lambda i: (i, 0, 0, 0)),
        out_shape=jax.ShapeDtypeStruct((width_y, slots, width_z, 2 * length), BF16),
        compiler_params=pltpu.CompilerParams(vmem_limit_bytes=56 * 2**20),
        name="spectra",
    )(ky, kz_col, state, cotangent)


def along_x_kernel(
    partner_ref, table_ref, spec_ref, *refs, first, chunks, block, width_y, span, parts
):
    out_refs, scratch = refs[:-1], refs[-1]
    step = pl.program_id(0)
    lanes = out_refs[0].shape[2]
    live = spec_ref.shape[1]
    pieces = [
        table_ref[partner_ref[k], first + j] for j in range(chunks) for k in range(parts)
    ]
    table = jnp.concatenate(pieces, axis=0)
    rows = table.shape[0]

    def one(k, carry):
        value = dot_nt(table, spec_ref[k])
        start = pl.multiple_of((step * block + k) * rows, 8)
        for v in range(lanes // LANES):
            if (v + 1) * LANES <= live:
                piece = value[:, v * LANES : (v + 1) * LANES]
                scratch[v, pl.ds(start, rows), :] = piece
            else:
                scratch[v, pl.ds(start, rows), :] = jnp.zeros((rows, LANES), F32)
                scratch[v, pl.ds(start, rows), pl.ds(0, live - v * LANES)] = value[:, v * LANES :]
        return carry

    lax.fori_loop(0, block, one, 0)

    @pl.when(step == pl.num_programs(0) - 1)
    def _():
        def move(x, carry):
            for target, out_ref in enumerate(out_refs):
                at = target * 2 * span + x
                for v in range(lanes // LANES):
                    sides = [
                        scratch[v, pl.ds(at + s * span, width_y, stride=rows), :] for s in range(2)
                    ]
                    block_rows = jnp.concatenate(sides, axis=0).astype(BF16)
                    out_ref[x, :, pl.ds(v * LANES, LANES)] = block_rows
            return carry

        lax.fori_loop(0, span, move, 0)


def along_x(partners, table, spectra, first, chunks):
    width_y, live, depth = spectra.shape
    parts = table.shape[0]
    span = table.shape[2] // 2
    rows = chunks * parts * 2 * span
    block = 8
    lanes = up_to(live, LANES)
    shape = (span, 2 * width_y, lanes)
    outs = pl.pallas_call(
        functools.partial(
            along_x_kernel,
            first=first,
            chunks=chunks,
            block=block,
            width_y=width_y,
            span=span,
            parts=parts,
        ),
        grid=(width_y // block,),
        in_specs=[
            pl.BlockSpec(memory_space=pltpu.SMEM),
            pl.BlockSpec(table.shape, lambda i: (0, 0, 0, 0)),
            pl.BlockSpec((block, live, depth), lambda i: (i, 0, 0)),
        ],
        out_specs=[pl.BlockSpec(shape, lambda i: (0, 0, 0))] * (parts * chunks),
        out_shape=[jax.ShapeDtypeStruct(shape, BF16)] * (parts * chunks),
        scratch_shapes=[pltpu.VMEM((lanes // LANES, width_y * rows, LANES), F32)],
        compiler_params=pltpu.CompilerParams(vmem_limit_bytes=58 * 2**20),
        cost_estimate=pl.CostEstimate(
            flops=2 * rows * live * depth * width_y * 2,
            bytes_accessed=2 * (width_y * live * depth + rows * width_y * lanes),
            transcendentals=0,
        ),
        name="along_x",
    )(partners, table, spectra)
    return [outs[j * parts : (j + 1) * parts] for j in range(chunks)]


def quads(low, high):
    upper = lax.broadcasted_iota(jnp.int32, low.shape, 1) < PATCH
    turned_high = pltpu.roll(high, PATCH, 1)
    turned_low = pltpu.roll(low, PATCH, 1)
    return jnp.where(upper, low, turned_high), jnp.where(upper, turned_low, high)


def halves(low, high):
    left = lax.broadcasted_iota(jnp.int32, low.shape, 1) < LANES // 2
    turned_high = pltpu.roll(high, LANES // 2, 1)
    turned_low = pltpu.roll(low, LANES // 2, 1)
    return jnp.where(left, low, turned_high), jnp.where(left, turned_low, high)


def physical_kernel(
    *refs,
    parts_x,
    parts_y,
    width_y,
    width_z,
    length,
    back_lanes,
):
    parts = parts_x * parts_y
    recv_refs, refs = refs[:parts], refs[parts:]
    physical_body(
        recv_refs, *refs, parts_x=parts_x, parts_y=parts_y, width_y=width_y,
        width_z=width_z, length=length, back_lanes=back_lanes,
    )


def physical_body(
    recv_refs,
    place_ref,
    ky_ref,
    kz_in_ref,
    kz_back_ref,
    ty_ref,
    tyb_ref,
    w_in_ref,
    w_in_t_ref,
    w_out_t_ref,
    bias_ref,
    *refs,
    parts_x,
    parts_y,
    width_y,
    width_z,
    length,
    back_lanes,
):
    z_refs = dict(zip(("uy", "uz", "ux", "wy", "wz", "fx", "fy", "fz", "wx"), refs[:9]))
    zb_ref = refs[9]
    parts = parts_x * parts_y
    out_refs, refs = refs[10 : 10 + parts], refs[10 + parts :]
    gin_ref, gout_ref = refs[:2]
    mid, vel, force, fields, fadj, back = refs[2:]
    rows = 2 * width_y
    in_lanes = recv_refs[0].shape[2]
    boxes = length // PATCH
    feats = 3 * PATCH * PATCH

    @pl.when(pl.program_id(0) == 0)
    def _():
        gin_ref[...] = jnp.zeros(gin_ref.shape, F32)
        gout_ref[...] = jnp.zeros(gout_ref.shape, F32)

    def section_y(dx, carry):
        for py in range(parts_y):
            whole = jnp.concatenate(
                [recv_refs[px * parts_y + py][dx] for px in range(parts_x)], axis=0
            )
            first = whole[:, :LANES].astype(F32)
            second = pltpu.roll(first, LANES - width_z, 1)
            mixed = ky_ref[...] * second - kz_in_ref[place_ref[1] ^ py] * first
            turned = []
            for px in range(parts_x):
                turned.append(-mixed[px * rows + width_y : (px + 1) * rows])
                turned.append(mixed[px * rows : px * rows + width_y])
            extra = jnp.concatenate(turned, axis=0).astype(BF16)
            mid[py, dx, :, pl.ds(0, in_lanes)] = dot(ty_ref[...], whole).astype(BF16)
            mid[py, dx, :, pl.ds(in_lanes, LANES)] = dot(ty_ref[...], extra).astype(BF16)
        return carry

    lax.fori_loop(0, PATCH, section_y, 0)

    def section_z(pair, carry):
        def field(name, dx):
            if name == "wx":
                vregs = [in_lanes // LANES]
            else:
                vregs = vregs_of(OUT_SLOTS.index(name), width_z)
            pieces = [
                mid[py, dx, pl.ds(t * length, length), pl.ds(v * LANES, LANES)]
                for py in range(parts_y)
                for t in range(2)
                for v in vregs
            ]
            table = [z_refs[name][place_ref[1] ^ py] for py in range(parts_y)]
            joined = jnp.concatenate(pieces, axis=1)
            return dot(joined, jnp.concatenate(table, axis=0)).astype(BF16)

        for kind, target in (("u", vel), ("f", force), ("w", None)):
            for slot, name in enumerate("xyz"):
                planes = []
                for i in range(2):
                    value = field(kind + name, 2 * pair + i)
                    fields["ufw".index(kind), slot, 2 * pair + i] = value
                    planes.append(value.astype(F32))
                if target is None:
                    continue
                rows_here = pl.ds(pl.multiple_of(slot * PATCH * PATCH + pair * 8, 8), 8)
                for half in range(length // LANES):
                    cut = slice(half * LANES, (half + 1) * LANES)
                    tiles = [value[:, cut].reshape(length // 8, 8, LANES) for value in planes]
                    for parity, value in enumerate(quads(*tiles)):
                        target[half, parity, :, rows_here, :] = value
        return carry

    lax.fori_loop(0, PATCH // 2, section_z, 0)

    def gather(source, at):
        per_dz = []
        for half in range(2):
            got = [
                halves(source[half, 0, at + p], source[half, 1, at + p])
                for p in range(PAIRS)
            ]
            for i in range(2):
                per_dz.append(jnp.concatenate([one[i] for one in got], axis=1))
        return jnp.concatenate(per_dz, axis=0).astype(BF16)

    hid = gin_ref.shape[0]
    unit = hid // HID_BLOCKS

    def closure(step, carry):
        at = step * PAIRS
        features = gather(vel, at)
        adjoints = gather(force, at)
        ones = jnp.ones((gin_ref.shape[1] - features.shape[0], features.shape[1]), BF16)
        extended = jnp.concatenate([features, ones], axis=0)
        pre_adjs = []
        for h in range(HID_BLOCKS):
            cut = pl.ds(h * unit, unit)
            bias = jnp.concatenate([bias_ref[cut, :]] * PAIRS, axis=1)
            pre = dot(w_in_ref[cut, :], features) + bias
            turned = jnp.tanh(0.5 * pre)
            sigma = 0.5 * turned + 0.5
            hidden = (pre * sigma).astype(BF16)
            hidden_adj = dot(w_out_t_ref[cut, :], adjoints)
            slope = FORCING * sigma + pre * ((0.5 * FORCING) * sigma * (1.0 - turned))
            pre_adj = (hidden_adj * slope).astype(BF16)
            gin_ref[cut, :] += dot_nt(pre_adj, extended)
            gout_ref[cut, :] += dot_nt(hidden, adjoints)
            pre_adjs.append(pre_adj)
        back_feat = dot(w_in_t_ref[...], jnp.concatenate(pre_adjs, axis=0))
        for half in range(2):
            low = back_feat[(2 * half) * feats : (2 * half + 1) * feats]
            high = back_feat[(2 * half + 1) * feats : (2 * half + 2) * feats]
            for p in range(PAIRS):
                cut = slice(p * LANES, (p + 1) * LANES)
                for parity, value in enumerate(halves(low[:, cut], high[:, cut])):
                    fadj[half, parity, at + p] = value
        return carry

    lax.fori_loop(0, boxes // (2 * PAIRS), closure, 0, unroll=UNROLL)

    back_vregs = back_lanes // LANES

    def section_back(pair, carry):
        adjoint = []
        for slot in range(3):
            rows_here = pl.ds(pl.multiple_of(slot * PATCH * PATCH + pair * 8, 8), 8)
            sides = [
                quads(fadj[half, 0, :, rows_here, :], fadj[half, 1, :, rows_here, :])
                for half in range(length // LANES)
            ]
            adjoint.append(
                [
                    jnp.concatenate([side[i].reshape(length, LANES) for side in sides], axis=1)
                    for i in range(2)
                ]
            )
        for i in range(2):
            one_plane(2 * pair + i, [value[i] for value in adjoint])
        return carry

    def one_plane(dx, adjoint):
        u, f, w = ([fields[k, c, dx].astype(F32) for c in range(3)] for k in range(3))
        named = {}
        for c, name in enumerate("xyz"):
            a, b = (c + 1) % 3, (c + 2) % 3
            turned = adjoint[c] + (w[a] * f[b] - w[b] * f[a])
            named["v" + name] = turned.astype(BF16)
            named["g" + name] = (f[a] * u[b] - f[b] * u[a]).astype(BF16)
        at = 0
        for group, names in enumerate(back_groups(width_z)):
            joined = jnp.concatenate([named[name] for name in names], axis=1)
            depth = joined.shape[1]
            for py in range(parts_y):
                table = zb_ref[place_ref[1] ^ py, pl.ds(at, depth), :]
                value = dot(joined, table).astype(BF16)
                for r in range(2):
                    piece = value[:, r * LANES : (r + 1) * LANES]
                    back[py, pl.ds(r * length, length), pl.ds(group * LANES, LANES)] = piece
            at += depth
        for py in range(parts_y):
            table = [tyb_ref[place_ref[0] ^ px] for px in range(parts_x)]
            value = dot(jnp.concatenate(table, axis=0), back[py])
            by_y = ky_ref[...] * value[:, back_lanes : back_lanes + LANES]
            by_z = value[:, back_lanes + LANES :]
            extra = []
            for v in range(back_vregs):
                here = kz_back_ref[place_ref[1] ^ py, v] * by_z
                if v == 0:
                    here = here + by_y
                extra.append(here)
            extra = jnp.concatenate(extra, axis=1)
            for px in range(parts_x):
                re = slice(px * rows, px * rows + width_y)
                im = slice(px * rows + width_y, (px + 1) * rows)
                total = jnp.concatenate(
                    [value[re, :back_lanes] - extra[im], value[im, :back_lanes] + extra[re]], axis=0
                )
                out_refs[px * parts_y + py][dx] = total.astype(BF16)

    lax.fori_loop(0, PATCH // 2, section_back, 0)


def back_groups(width_z):
    names = [{"a": "v", "g": "g"}[slot[0]] + slot[1] for slot in BACK_SLOTS]
    lanes = up_to(len(BACK_SLOTS) * width_z, LANES)
    groups = []
    for v in range(lanes // LANES):
        groups.append([n for slot, n in enumerate(names) if v in vregs_of(slot, width_z)])
    groups.append(["gz", "gx"])
    groups.append(["gy", "gx"])
    return groups


def back_table(width_z, length, parts_y):
    names = [{"a": "v", "g": "g"}[slot[0]] + slot[1] for slot in BACK_SLOTS]
    lanes = up_to(len(BACK_SLOTS) * width_z, LANES)
    groups = back_groups(width_z)
    order = box_order(length)

    def piece(slot, vreg, py, sign):
        modes, inside = lane_modes(slot, width_z, lanes, py * width_z)
        cut = slice(vreg * LANES, (vreg + 1) * LANES)
        cosine, sine = angles(order, modes[cut], length)
        keep = sign * inside[cut].astype(np.float32)[None, :]
        return np.concatenate([cosine * keep, -sine * keep], axis=1)

    ky_slots = {"gz": (BACK_SLOTS.index("ax"), 1.0), "gx": (BACK_SLOTS.index("az"), -1.0)}
    kz_slots = {"gy": (BACK_SLOTS.index("ax"), -1.0), "gx": (BACK_SLOTS.index("ay"), 1.0)}
    tables = []
    for py in range(parts_y):
        rows = []
        for v, group in enumerate(groups[:-2]):
            rows += [piece(names.index(n), v, py, 1.0) for n in group]
        for which, group in ((ky_slots, groups[-2]), (kz_slots, groups[-1])):
            for n in group:
                slot, sign = which[n]
                rows.append(sum(piece(slot, v, py, sign) for v in vregs_of(slot, width_z)))
        tables.append(np.concatenate(rows, axis=0))
    return jnp.asarray(np.stack(tables), BF16)


def out_table(slot, width_z, length, parts_y):
    lanes = (vregs_of(slot, width_z)[-1] + 1) * LANES
    order = box_order(length)
    tables = []
    for py in range(parts_y):
        modes, inside = lane_modes(slot, width_z, lanes, py * width_z)
        cosine, sine = angles(modes, order, length)
        keep = inside.astype(np.float32)[:, None]
        rows = []
        for value in (cosine, -sine):
            for v in vregs_of(slot, width_z):
                rows.append((value * keep)[v * LANES : (v + 1) * LANES])
        tables.append(np.concatenate(rows, axis=0))
    return jnp.asarray(np.stack(tables), BF16)


def physical(recv, place, ky_rows, kz_in, kz_back, tables, weights, grid_sizes, back_lanes):
    parts_x, parts_y, width_y, width_z, length = grid_sizes
    parts = parts_x * parts_y
    span, rows, in_lanes = recv[0].shape
    hid = weights[0].shape[0]
    feat = weights[0].shape[1]
    t_y, t_yb, z_tables, z_back = tables

    def whole(array):
        return pl.BlockSpec(array.shape, lambda i: (0,) * array.ndim)

    small = [ky_rows, kz_in, kz_back, t_y, t_yb, *weights, *z_tables, z_back]
    feat_pad = up_to(feat + 1, 2 * LANES)
    boxed = (length // LANES, 2, length // (2 * PATCH), 3 * PATCH * PATCH, LANES)
    flops = 2 * span * parts_y * (2 * length) * (parts_x * rows) * (in_lanes + LANES)
    flops += 2 * 5 * hid * feat * (span * length * length // PATCH**3)
    flops += 2 * span * length * length * length * (9 * 2 + 20)
    return pl.pallas_call(
        functools.partial(
            physical_kernel,
            parts_x=parts_x,
            parts_y=parts_y,
            width_y=width_y,
            width_z=width_z,
            length=length,
            back_lanes=back_lanes,
        ),
        grid=(span // PATCH,),
        in_specs=[pl.BlockSpec((PATCH, rows, in_lanes), lambda i: (i, 0, 0))] * parts
        + [pl.BlockSpec(memory_space=pltpu.SMEM)]
        + [whole(a) for a in small],
        out_specs=[pl.BlockSpec((PATCH, rows, back_lanes), lambda i: (i, 0, 0))] * parts
        + [
            pl.BlockSpec((hid, feat_pad), lambda i: (0, 0)),
            pl.BlockSpec((hid, feat), lambda i: (0, 0)),
        ],
        out_shape=[jax.ShapeDtypeStruct((span, rows, back_lanes), BF16)] * parts
        + [
            jax.ShapeDtypeStruct((hid, feat_pad), F32),
            jax.ShapeDtypeStruct((hid, feat), F32),
        ],
        scratch_shapes=[
            pltpu.VMEM((parts_y, PATCH, 2 * length, in_lanes + LANES), BF16),
            pltpu.VMEM(boxed, F32),
            pltpu.VMEM(boxed, F32),
            pltpu.VMEM((3, 3, PATCH, length, length), BF16),
            pltpu.VMEM(boxed, F32),
            pltpu.VMEM((parts_y, 2 * length, back_lanes + 2 * LANES), BF16),
        ],
        compiler_params=pltpu.CompilerParams(vmem_limit_bytes=58 * 2**20),
        cost_estimate=pl.CostEstimate(
            flops=flops, bytes_accessed=4 * parts * recv[0].size, transcendentals=0
        ),
        name="physical",
    )(*recv, place, *small)


def final_kernel(
    partner_ref, ky_ref, kz_ref, table_ref, cot_ref, *refs, steps_in, block, width_y, width_z, length
):
    out_ref, scratch, turned = refs[-3:]
    recv_refs = refs[:-3]
    parts = partner_ref.shape[0]
    step = pl.program_id(0)
    rows = 2 * width_y
    lanes = recv_refs[0].shape[2]

    @pl.when(step < steps_in)
    def _():
        for j, recv_ref in enumerate(recv_refs):
            source = partner_ref[j % parts]
            x = source * (length // parts) + (j // parts) * steps_in + step
            at = pl.multiple_of(x * rows, 8)
            value = recv_ref[0].astype(F32)
            for v in range(lanes // LANES):
                scratch[v, pl.ds(at, rows), :] = value[:, v * LANES : (v + 1) * LANES]

    @pl.when(step >= steps_in)
    def _():
        cutoff = float(length // 3)
        wave_z = kz_ref[...]
        counter = lax.broadcasted_iota(jnp.int32, wave_z.shape, 1)
        wave_x = jnp.where(counter < length // 2, counter, counter - length).astype(F32)
        plane = wave_x * wave_x + wave_z * wave_z
        inside = (jnp.abs(wave_x) <= cutoff) & (wave_z <= cutoff)
        weight = jnp.where(wave_z == 0.0, 1.0, 2.0).astype(F32)

        def one(k, carry):
            ky = (step - steps_in) * block + k
            pieces = []
            for v in range(lanes // LANES):
                parts_s = [
                    scratch[v, pl.ds(ky + s * width_y, length, stride=rows), :] for s in range(2)
                ]
                pieces.append(jnp.concatenate(parts_s, axis=0))
            gathered = jnp.concatenate(pieces, axis=1).astype(BF16)
            turned[...] = dot_tn(gathered, table_ref[...])
            wave_y = ky_ref[ky]
            kept = jnp.where(inside & (jnp.abs(wave_y) <= cutoff), 1.0, 0.0).astype(F32)
            damped = jnp.exp(-NU_DT * (plane + wave_y * wave_y))
            scale = kept * weight

            def part(name, t):
                at = BACK_SLOTS.index(name) * width_z
                return turned[pl.ds(at, width_z), pl.ds(t * length, length)]

            for t in range(2):
                sign = -1.0 if t == 0 else 1.0
                ax = part("ax", t)
                ay = part("ay", t) - sign * wave_x * part("gz", 1 - t)
                az = part("az", t) + sign * wave_x * part("gy", 1 - t)
                for c, value in enumerate((ax, ay, az)):
                    out_ref[c, t, k] = damped * cot_ref[c, t, k] + scale * value
            return carry

        lax.fori_loop(0, block, one, 0)


def finish(partners, ky, kz_col, table, cotangent, received):
    _, _, width_y, width_z, length = cotangent.shape
    span, rows, lanes = received[0].shape
    block = 8
    steps_in = span
    steps = steps_in + width_y // block
    spec = pl.BlockSpec(
        (3, 2, block, width_z, length), lambda i: (0, 0, jnp.maximum(i - steps_in, 0), 0, 0)
    )
    recv_spec = pl.BlockSpec((1, rows, lanes), lambda i: (jnp.minimum(i, steps_in - 1), 0, 0))
    return pl.pallas_call(
        functools.partial(
            final_kernel,
            steps_in=steps_in,
            block=block,
            width_y=width_y,
            width_z=width_z,
            length=length,
        ),
        grid=(steps,),
        in_specs=[
            pl.BlockSpec(memory_space=pltpu.SMEM),
            pl.BlockSpec(memory_space=pltpu.SMEM),
            pl.BlockSpec((width_z, length), lambda i: (0, 0)),
            pl.BlockSpec(table.shape, lambda i: (0, 0)),
            spec,
        ]
        + [recv_spec] * len(received),
        out_specs=spec,
        out_shape=jax.ShapeDtypeStruct(cotangent.shape, F32),
        scratch_shapes=[
            pltpu.VMEM((lanes // LANES, length * rows, LANES), F32),
            pltpu.VMEM((lanes, 2 * length), F32),
        ],
        compiler_params=pltpu.CompilerParams(vmem_limit_bytes=60 * 2**20),
        name="finish",
    )(partners, ky, kz_col, table, cotangent, *received)


def shards(state, cotangent, w_in, b_in, w_out):
    width_y, width_z, length = state.shape[2:]
    parts_x = lax.axis_size("px")
    parts_y = lax.axis_size("py")
    parts = parts_x * parts_y
    slab = length // parts
    chunks = MAX_CHUNKS
    while chunks > 1 and slab % (chunks * PATCH) != 0:
        chunks //= 2
    span = slab // chunks
    ky_count = width_y * parts_x
    hid, feat = w_in.shape

    own_x = lax.axis_index("px")
    own_y = lax.axis_index("py")
    own = own_x * parts_y + own_y
    partners = own ^ jnp.arange(parts, dtype=jnp.int32)
    partners_x = own_x ^ jnp.arange(parts_x, dtype=jnp.int32)
    local_y = jnp.arange(width_y, dtype=jnp.int32)
    ky_ids = own_x * width_y + local_y
    kz_ids = own_y * width_z + jnp.arange(width_z, dtype=jnp.int32)
    ky = signed(ky_ids, ky_count)
    kz_col = jnp.broadcast_to(kz_ids.astype(F32)[:, None], (width_z, length))

    everything = np.arange(length)
    cosine, sine = angles(everything, everything, length)
    both = np.stack(
        [np.concatenate([cosine, -sine], axis=1), np.concatenate([sine, cosine], axis=1)]
    )
    x_back = jnp.asarray(both.reshape(2 * length, 2 * length), BF16)
    x_rows = both.reshape(2, parts, chunks, span, 2 * length).transpose(1, 2, 0, 3, 4)
    x_rows = jnp.asarray(x_rows.reshape(parts, chunks, 2 * span, 2 * length), BF16)

    ky_modes = mode_ids(ky_count, length)
    cosine, sine = angles(everything, ky_modes, length)
    cosine = cosine.reshape(length, parts_x, width_y)
    sine = sine.reshape(length, parts_x, width_y)
    t_y = np.stack(
        [np.concatenate([cosine, -sine], axis=2), np.concatenate([sine, cosine], axis=2)]
    )
    t_yb = jnp.asarray(t_y.reshape(2 * length, parts_x, -1).transpose(1, 2, 0), BF16)
    t_y = jnp.asarray(t_y.reshape(2 * length, parts_x, -1), BF16)
    t_y = jnp.take(t_y, partners_x, axis=1).reshape(2 * length, -1)

    z_tables = [out_table(slot, width_z, length, parts_y) for slot in range(len(OUT_SLOTS))]
    z_tables.append(z_tables[0])
    z_back = back_table(width_z, length, parts_y)

    back_lanes = up_to(len(BACK_SLOTS) * width_z, LANES)
    ky_order = (partners_x[:, None] * width_y + local_y[None, :]).astype(jnp.int32)
    ky_rows = signed(ky_order, ky_count).reshape(parts_x, 1, width_y, 1)
    ky_rows = jnp.broadcast_to(ky_rows, (parts_x, 2, width_y, LANES)).reshape(-1, LANES)
    kz_in, kz_back = [], []
    for py in range(parts_y):
        modes, inside = lane_modes(0, width_z, LANES, py * width_z)
        kz_in.append(np.where(inside, modes, 0)[None, :])
        total = np.zeros((back_lanes,))
        for name in ("ax", "ay"):
            slot = BACK_SLOTS.index(name)
            modes, inside = lane_modes(slot, width_z, back_lanes, py * width_z)
            total = total + np.where(inside, modes, 0)
        kz_back.append(total.reshape(-1, 1, LANES))
    kz_in = jnp.asarray(np.stack(kz_in), F32)
    kz_back = jnp.asarray(np.stack(kz_back), F32)

    units = hid // parts

    def turn(weight):
        split = weight.reshape(parts, units, 3, PATCH, PATCH, PATCH)[partners]
        return split.transpose(0, 1, 5, 2, 3, 4).reshape(hid, feat)

    w_in_f = turn(w_in)
    w_out_t = turn(w_out.T)
    bias = b_in.reshape(parts, units)[partners].reshape(hid, 1)
    bias = jnp.broadcast_to(bias, (hid, LANES))
    weights = (w_in_f, w_in_f.T, w_out_t, bias)

    def exchange(arrays):
        moved = [arrays[0]]
        for k in range(1, parts):
            pairs = [(i, i ^ k) for i in range(parts)]
            moved.append(lax.ppermute(arrays[k], ("px", "py"), pairs))
        return moved

    spectra = make_spectra(ky, kz_col, state, cotangent)
    spectra = spectra.reshape(width_y, -1, 2 * length)
    arrived = []
    groups = ((0, 1), (1, 1), (2, 2)) if chunks == 4 else tuple((j, 1) for j in range(chunks))
    for first, count in groups:
        outs = along_x(partners, x_rows, spectra, first, count)
        for sent in outs:
            arrived.append(exchange(sent))
    place = jnp.stack([own_x, own_y]).astype(jnp.int32)
    grid_sizes = (parts_x, parts_y, width_y, width_z, length)
    tables = (t_y, t_yb, z_tables, z_back)
    returned = []
    grads = 0.0
    for recv in arrived:
        *sent, gin, gout = physical(
            recv, place, ky_rows, kz_in, kz_back, tables, weights, grid_sizes, back_lanes
        )
        returned.append(exchange(sent))
        grads = grads + jnp.concatenate([gin, gout], axis=1)
    grads = sum(exchange([grads[k * units : (k + 1) * units] for k in range(parts)]))

    received = [array for chunk in returned for array in chunk]
    state_grad = finish(partners, ky, kz_col, x_back, cotangent, received)

    pad = up_to(feat + 1, 2 * LANES)

    def unturn(weight):
        split = weight.reshape(units, PATCH, 3, PATCH, PATCH)
        return split.transpose(0, 2, 3, 4, 1).reshape(units, feat)

    grad_in = unturn(grads[:, :feat])
    grad_bias = grads[:, feat][None, :]
    grad_out = FORCING * unturn(grads[:, pad:]).T
    return state_grad, grad_in, grad_out, grad_bias


def solution(mesh):
    return jax.shard_map(
        shards,
        mesh=mesh,
        in_specs=(
            P("rep", None, "px", "py", None),
            P("rep", None, "px", "py", None),
            P(),
            P(),
            P(),
        ),
        out_specs=(
            P("rep", None, "px", "py", None),
            P(("px", "py"), "rep"),
            P("rep", ("px", "py")),
            P("rep", ("px", "py")),
        ),
        check_vma=False,
    )
```

time: 728 us -> 605 us (0.83)
  blocking collectives: 139 us -> 0 us
  waiting for transfers between devices: 67 us -> 169 us
  Pallas kernels: 423 us -> 342 us
  starting transfers between devices: 23.2 us -> 66.7 us
  other arithmetic: 45.8 us -> 4.24 us
    ppermute x0 -> x63, waiting for transfers between devices: none -> 169 us  [exchange(): moved.append(lax.ppermute(arrays[k], ('px', 'py'), pairs))]
    all_to_all x4 -> x0, blocking collectives: 139 us -> none  [the longest x3 121 us: shards(): returned.append(exchange(sent))]
    all_to_all x5 -> x0, waiting for transfers between devices: 67 us -> none  [the longest x4 36.8 us: shards(): arrived.append(exchange(along_x(table, spectra, parts, span)))]
    ppermute x0 -> x63, starting transfers between devices: none -> 66.7 us  [exchange(): moved.append(lax.ppermute(arrays[k], ('px', 'py'), pairs))]
    pallas_call x4, Pallas kernels: 257 us -> 194 us  [physical(): pl.pallas_call(functools.partial(physical_kernel, parts_x=parts_x, parts_...]
    all_to_all x5 -> x0, starting transfers between devices: 23.2 us -> none  [the longest x4 19.6 us: shards(): arrived.append(exchange(along_x(table, spectra, parts, span)))]
    another operation x12 -> x1, other arithmetic: 20.5 us -> 0.59 us  [shards(): place = jnp.stack([own_x, own_y]).astype(jnp.int32)]
    pallas_call x4 -> x3, Pallas kernels: 98.9 us -> 81.1 us  [along_x(): pl.pallas_call(functools.partial(along_x_kernel, first=first, chunks=chun...]
  transfers between devices with their start and end apart: 5 -> 63, of which waited for: 4 -> 27; matrix products, arithmetic and copies ran while one was open for 8% -> 2% of each run, Pallas kernels for 37% -> 32%
where the time goes in v2:
time: 605 us; the launch traced here: 598 us
  Pallas kernels  342 us (57%)
  waiting for transfers between devices  169 us (28%)
  starting transfers between devices  66.7 us (11%)
  local copies, waits for them, and re-layouts  13.9 us (2%)
    pallas_call x4, Pallas kernels, physical(): pl.pallas_call(functools.partial(physical_kernel, parts_x=parts_x, parts_...  194 us
    ppermute x63, waiting for transfers between devices, exchange(): moved.append(lax.ppermute(arrays[k], ('px', 'py'), pairs))  169 us
    pallas_call x3, Pallas kernels, along_x(): pl.pallas_call(functools.partial(along_x_kernel, first=first, chunks=chun...  81.1 us
    ppermute x63, starting transfers between devices, exchange(): moved.append(lax.ppermute(arrays[k], ('px', 'py'), pairs))  66.7 us
    pallas_call x1, Pallas kernels, finish(): pl.pallas_call(functools.partial(final_kernel, steps_in=steps_in, block=b...  48.7 us
    pallas_call x1, Pallas kernels, make_spectra(): pl.pallas_call(functools.partial(spectra_kernel, block=block, length=leng...  18 us
  transfers between devices with their start and end apart: 63, of which 27 were waited for; matrix products, arithmetic and copies ran while one was open for 2% of the time, Pallas kernels for 32%

profile of v2, /device:TPU:0, one launch (start us, length us, event | category | flops | bytes accessed | tf_op | source)
XLA Modules:
  0.0 597.6 jit_solution(4475390000764818777)
XLA Ops:
  2.3 18.0 %spectra.1 = bf16[48,8,48,512]{3,2,1,0:T(8,128)(2,1)} custom-call(f32[48]{0:T(128)} %fusion.9.ky_ref, f32[48,256]{1,0:T(8,128)} %broadcast_in_dim.41.kz_ref, f32[3,2,48,48,256]{4,3,2,1,0:T(8,128)} %state_ref.1, f32[3,2,48,48,256]{4,3,2,1,0:T(8,128)} %cot_ref.3), custom_call_target="tpu_custom_call" | custom-call | tf_op jit(solution)/shard_map/spectra/pallas_call | solution.py:120
  20.3 32.7 %along_x.5 = (bf16[8,96,384]{2,1,0:T(8,128)(2,1)}, bf16[8,96,384]{2,1,0:T(8,128)(2,1)}, bf16[8,96,384]{2,1,0:T(8,128)(2,1)}, bf16[8,96,384]{2,1,0:T(8,128)(2,1)}...) custom-call(s32[8]{0:T(128)} %iota_xor_fusion.1.partner_ref, ...), custom_call_target="tpu_custom_call" | custom-call | flops 9663676416 | bytes 28311552 | tf_op jit(solution)/shard_map/along_x/pallas_call | solution.py:187
  61.4 9.0 %collective-permute-done.42.refs_1_ = bf16[8,96,384]{2,1,0:T(8,128)(2,1)S(1)} collective-permute-done((bf16[8,96,384]{2,1,0:T(8,128)(2,1)}, bf16[8,96,384]{2,1,0:T(8,128)(2,1)S(1)}, u32[]{:S(2)}, u32[]{:S(2)}) %collective-permute-start.42) | collective-permute-done | bytes 589856 | tf_op jit(solution)/shard_map/ppermute | solution.py:739
  73.6 20.6 %collective-permute-done.44.refs_3_ = bf16[8,96,384]{2,1,0:T(8,128)(2,1)S(1)} collective-permute-done((bf16[8,96,384]{2,1,0:T(8,128)(2,1)}, bf16[8,96,384]{2,1,0:T(8,128)(2,1)S(1)}, u32[]{:S(2)}, u32[]{:S(2)}) %collective-permute-start.44) | collective-permute-done | bytes 589856 | tf_op jit(solution)/shard_map/ppermute | solution.py:739
  95.5 24.2 %along_x.4 = (bf16[8,96,384]{2,1,0:T(8,128)(2,1)}, bf16[8,96,384]{2,1,0:T(8,128)(2,1)}, bf16[8,96,384]{2,1,0:T(8,128)(2,1)}, bf16[8,96,384]{2,1,0:T(8,128)(2,1)}...) custom-call(s32[8]{0:T(128)} %iota_xor_fusion.1.partner_ref, ...), custom_call_target="tpu_custom_call" | custom-call | flops 4831838208 | bytes 23592960 | tf_op jit(solution)/shard_map/along_x/pallas_call | solution.py:187
  131.8 24.3 %along_x.3 = (bf16[8,96,384]{2,1,0:T(8,128)(2,1)}, bf16[8,96,384]{2,1,0:T(8,128)(2,1)}, bf16[8,96,384]{2,1,0:T(8,128)(2,1)}, bf16[8,96,384]{2,1,0:T(8,128)(2,1)}...) custom-call(s32[8]{0:T(128)} %iota_xor_fusion.1.partner_ref, ...), custom_call_target="tpu_custom_call" | custom-call | flops 4831838208 | bytes 23592960 | tf_op jit(solution)/shard_map/along_x/pallas_call | solution.py:187
  164.8 48.6 %physical.7 = (bf16[8,96,256]{2,1,0:T(8,128)(2,1)}, bf16[8,96,256]{2,1,0:T(8,128)(2,1)}, bf16[8,96,256]{2,1,0:T(8,128)(2,1)}, bf16[8,96,256]{2,1,0:T(8,128)(2,1)...) custom-call(bf16[8,96,384]{2,1,0:T(8,128)(2,1)} %get-tuple-element.1, ...), custom_call_target="tpu_custom_call" | custom-call | flops 21474836480 | bytes 9437184 | tf_op jit(solution)/shard_map/physical/pallas_call | solution.py:518
  218.6 48.7 %physical.6 = (bf16[8,96,256]{2,1,0:T(8,128)(2,1)}, bf16[8,96,256]{2,1,0:T(8,128)(2,1)}, bf16[8,96,256]{2,1,0:T(8,128)(2,1)}, bf16[8,96,256]{2,1,0:T(8,128)(2,1)...) custom-call(bf16[8,96,384]{2,1,0:T(8,128)(2,1)} %get-tuple-element.1, ...), custom_call_target="tpu_custom_call" | custom-call | flops 21474836480 | bytes 9437184 | tf_op jit(solution)/shard_map/physical/pallas_call | solution.py:518
  272.6 48.1 %physical.5 = (bf16[8,96,256]{2,1,0:T(8,128)(2,1)}, bf16[8,96,256]{2,1,0:T(8,128)(2,1)}, bf16[8,96,256]{2,1,0:T(8,128)(2,1)}, bf16[8,96,256]{2,1,0:T(8,128)(2,1)...) custom-call(bf16[8,96,384]{2,1,0:T(8,128)(2,1)} %get-tuple-element.9, ...), custom_call_target="tpu_custom_call" | custom-call | flops 21474836480 | bytes 9437184 | tf_op jit(solution)/shard_map/physical/pallas_call | solution.py:518
  322.5 48.4 %physical.4 = (bf16[8,96,256]{2,1,0:T(8,128)(2,1)}, bf16[8,96,256]{2,1,0:T(8,128)(2,1)}, bf16[8,96,256]{2,1,0:T(8,128)(2,1)}, bf16[8,96,256]{2,1,0:T(8,128)(2,1)...) custom-call(bf16[8,96,384]{2,1,0:T(8,128)(2,1)} %get-tuple-element.7, ...), custom_call_target="tpu_custom_call" | custom-call | flops 21474836480 | bytes 9437184 | tf_op jit(solution)/shard_map/physical/pallas_call | solution.py:518
  380.7 17.0 %collective-permute-done.58 = f32[64,448]{1,0:T(8,128)S(1)} collective-permute-done((f32[64,448]{1,0:T(8,128)S(1)}, f32[64,448]{1,0:T(8,128)S(1)}, u32[]{:S(2)}, u32[]{:S(2)}) %collective-permute-start.58) | collective-permute-done | bytes 114720 | tf_op jit(solution)/shard_map/ppermute | solution.py:739
  400.0 5.0 collective-permute-done.60
  419.4 7.9 %collective-permute-done.53.refs_29_ = bf16[8,96,256]{2,1,0:T(8,128)(2,1)S(1)} collective-permute-done((bf16[8,96,256]{2,1,0:T(8,128)(2,1)S(1)}, bf16[8,96,256]{2,1,0:T(8,128)(2,1)S(1)}, u32[]{:S(2)}, u32[]{:S(2)}) %collective-permute-start.53) | collective-permute-done | bytes 393248 | tf_op jit(solution)/shard_map/ppermute | solution.py:739
  428.5 7.2 %collective-permute-done.54.refs_30_ = bf16[8,96,256]{2,1,0:T(8,128)(2,1)S(1)} collective-permute-done((bf16[8,96,256]{2,1,0:T(8,128)(2,1)S(1)}, bf16[8,96,256]{2,1,0:T(8,128)(2,1)S(1)}, u32[]{:S(2)}, u32[]{:S(2)}) %collective-permute-start.54) | collective-permute-done | bytes 393248 | tf_op jit(solution)/shard_map/ppermute | solution.py:739
  437.0 8.4 %collective-permute-done.55.refs_31_ = bf16[8,96,256]{2,1,0:T(8,128)(2,1)S(1)} collective-permute-done((bf16[8,96,256]{2,1,0:T(8,128)(2,1)S(1)}, bf16[8,96,256]{2,1,0:T(8,128)(2,1)S(1)}, u32[]{:S(2)}, u32[]{:S(2)}) %collective-permute-start.55) | collective-permute-done | bytes 393248 | tf_op jit(solution)/shard_map/ppermute | solution.py:739
  453.2 7.9 %collective-permute-done.39.refs_21_ = bf16[8,96,256]{2,1,0:T(8,128)(2,1)S(1)} collective-permute-done((bf16[8,96,256]{2,1,0:T(8,128)(2,1)S(1)}, bf16[8,96,256]{2,1,0:T(8,128)(2,1)S(1)}, u32[]{:S(2)}, u32[]{:S(2)}) %collective-permute-start.39) | collective-permute-done | bytes 393248 | tf_op jit(solution)/shard_map/ppermute | solution.py:739
  462.3 7.2 %collective-permute-done.40.refs_22_ = bf16[8,96,256]{2,1,0:T(8,128)(2,1)S(1)} collective-permute-done((bf16[8,96,256]{2,1,0:T(8,128)(2,1)S(1)}, bf16[8,96,256]{2,1,0:T(8,128)(2,1)S(1)}, u32[]{:S(2)}, u32[]{:S(2)}) %collective-permute-start.40) | collective-permute-done | bytes 393248 | tf_op jit(solution)/shard_map/ppermute | solution.py:739
  470.8 8.4 %collective-permute-done.41.refs_23_ = bf16[8,96,256]{2,1,0:T(8,128)(2,1)S(1)} collective-permute-done((bf16[8,96,256]{2,1,0:T(8,128)(2,1)S(1)}, bf16[8,96,256]{2,1,0:T(8,128)(2,1)S(1)}, u32[]{:S(2)}, u32[]{:S(2)}) %collective-permute-start.41) | collective-permute-done | bytes 393248 | tf_op jit(solution)/shard_map/ppermute | solution.py:739
  496.8 6.5 %collective-permute-done.26.refs_14_ = bf16[8,96,256]{2,1,0:T(8,128)(2,1)S(1)} collective-permute-done((bf16[8,96,256]{2,1,0:T(8,128)(2,1)S(1)}, bf16[8,96,256]{2,1,0:T(8,128)(2,1)S(1)}, u32[]{:S(2)}, u32[]{:S(2)}) %collective-permute-start.26) | collective-permute-done | bytes 393248 | tf_op jit(solution)/shard_map/ppermute | solution.py:739
  504.3 8.6 %collective-permute-done.27.refs_15_ = bf16[8,96,256]{2,1,0:T(8,128)(2,1)S(1)} collective-permute-done((bf16[8,96,256]{2,1,0:T(8,128)(2,1)S(1)}, bf16[8,96,256]{2,1,0:T(8,128)(2,1)S(1)}, u32[]{:S(2)}, u32[]{:S(2)}) %collective-permute-start.27) | collective-permute-done | bytes 393248 | tf_op jit(solution)/shard_map/ppermute | solution.py:739
  513.2 7.5 %collective-permute-done.10.refs_4_ = bf16[8,96,256]{2,1,0:T(8,128)(2,1)S(1)} collective-permute-done((bf16[8,96,256]{2,1,0:T(8,128)(2,1)S(1)}, bf16[8,96,256]{2,1,0:T(8,128)(2,1)S(1)}, u32[]{:S(2)}, u32[]{:S(2)}) %collective-permute-start.10) | collective-permute-done | bytes 393248 | tf_op jit(solution)/shard_map/ppermute | solution.py:739
  520.7 7.9 %collective-permute-done.11.refs_5_ = bf16[8,96,256]{2,1,0:T(8,128)(2,1)S(1)} collective-permute-done((bf16[8,96,256]{2,1,0:T(8,128)(2,1)S(1)}, bf16[8,96,256]{2,1,0:T(8,128)(2,1)S(1)}, u32[]{:S(2)}, u32[]{:S(2)}) %collective-permute-start.11) | collective-permute-done | bytes 393248 | tf_op jit(solution)/shard_map/ppermute | solution.py:739
  537.2 9.0 %collective-permute-done.13.refs_7_ = bf16[8,96,256]{2,1,0:T(8,128)(2,1)} collective-permute-done((bf16[8,96,256]{2,1,0:T(8,128)(2,1)}, bf16[8,96,256]{2,1,0:T(8,128)(2,1)}, u32[]{:S(2)}, u32[]{:S(2)}) %collective-permute-start.13) | collective-permute-done | bytes 393248 | tf_op jit(solution)/shard_map/ppermute | solution.py:739
  548.7 48.7 %finish.1 = f32[3,2,48,48,256]{4,3,2,1,0:T(8,128)} custom-call(s32[8]{0:T(128)} %iota_xor_fusion.1.partner_ref, f32[48]{0:T(128)} %fusion.9.ky_ref, f32[48,256]{1,0:T(8,128)} %broadcast_in_dim.41.kz_ref, bf16[512,512]{1,0:T(8,128)(2,1)} %constant.72.clone.table_ref, f32[3,2,48,48,256]{4,3,2,1,0:T(8,128)} %cot_ref.3, ...), custom_call_target="tpu_custom_call" | custom-call | tf_op jit(solution)/shard_map/finish/pallas_call | solution.py:629
  (314 shorter events, 116.3 us)
Async XLA Ops:
  56.0 38.2 %collective-permute-start.44 = (bf16[8,96,384]{2,1,0:T(8,128)(2,1)}, bf16[8,96,384]{2,1,0:T(8,128)(2,1)S(1)}, u32[]{:S(2)}, u32[]{:S(2)}) collective-permute-start(bf16[8,96,384]{2,1,0:T(8,128)(2,1)} %get-tuple-element.127), channel_id=1, source_target_pairs={{0,3},{1,2},{2,1},{3,0},{4,7},{5,6},{6,5},{7,4},{8,11},{9,10},{10,... | collective-permute-start | bytes 1769480 | tf_op jit(solution)/shard_map/ppermute | solution.py:739
  56.2 63.5 %collective-permute-start.45 = (bf16[8,96,384]{2,1,0:T(8,128)(2,1)}, bf16[8,96,384]{2,1,0:T(8,128)(2,1)}, u32[]{:S(2)}, u32[]{:S(2)}) collective-permute-start(bf16[8,96,384]{2,1,0:T(8,128)(2,1)} %get-tuple-element.128), channel_id=1, source_target_pairs={{0,4},{1,5},{2,6},{3,7},{4,0},{5,1},{6,2},{7,3},{8,12},{9,13},{10,... | collective-permute-start | bytes 1769480 | tf_op jit(solution)/shard_map/ppermute | solution.py:739
  58.1 62.6 %collective-permute-start.46 = (bf16[8,96,384]{2,1,0:T(8,128)(2,1)}, bf16[8,96,384]{2,1,0:T(8,128)(2,1)}, u32[]{:S(2)}, u32[]{:S(2)}) collective-permute-start(bf16[8,96,384]{2,1,0:T(8,128)(2,1)} %get-tuple-element.129), channel_id=1, source_target_pairs={{0,5},{1,4},{2,7},{3,6},{4,1},{5,0},{6,3},{7,2},{8,13},{9,12},{10,... | collective-permute-start | bytes 1769480 | tf_op jit(solution)/shard_map/ppermute | solution.py:739
  70.4 50.5 %collective-permute-start.47 = (bf16[8,96,384]{2,1,0:T(8,128)(2,1)}, bf16[8,96,384]{2,1,0:T(8,128)(2,1)S(1)}, u32[]{:S(2)}, u32[]{:S(2)}) collective-permute-start(bf16[8,96,384]{2,1,0:T(8,128)(2,1)} %get-tuple-element.130), channel_id=1, source_target_pairs={{0,6},{1,7},{2,4},{3,5},{4,2},{5,3},{6,0},{7,1},{8,14},{9,15},{10,... | collective-permute-start | bytes 1769480 | tf_op jit(solution)/shard_map/ppermute | solution.py:739
  70.4 52.0 %collective-permute-start.48 = (bf16[8,96,384]{2,1,0:T(8,128)(2,1)}, bf16[8,96,384]{2,1,0:T(8,128)(2,1)S(1)}, u32[]{:S(2)}, u32[]{:S(2)}) collective-permute-start(bf16[8,96,384]{2,1,0:T(8,128)(2,1)} %get-tuple-element.131), channel_id=1, source_target_pairs={{0,7},{1,6},{2,5},{3,4},{4,3},{5,2},{6,1},{7,0},{8,15},{9,14},{10,... | collective-permute-start | bytes 1769480 | tf_op jit(solution)/shard_map/ppermute | solution.py:739
  156.1 57.3 %collective-permute-start.34 = (bf16[8,96,384]{2,1,0:T(8,128)(2,1)S(1)}, bf16[8,96,384]{2,1,0:T(8,128)(2,1)}, u32[]{:S(2)}, u32[]{:S(2)}) collective-permute-start(bf16[8,96,384]{2,1,0:T(8,128)(2,1)S(1)} %copy-done.35), channel_id=1, source_target_pairs={{0,7},{1,6},{2,5},{3,4},{4,3},{5,2},{6,1},{7,0},{8,15},{9,14},{10,... | collective-permute-start | bytes 1769480 | tf_op jit(solution)/shard_map/ppermute | solution.py:739
  156.8 58.3 %collective-permute-start.14 = (bf16[8,96,384]{2,1,0:T(8,128)(2,1)}, bf16[8,96,384]{2,1,0:T(8,128)(2,1)}, u32[]{:S(2)}, u32[]{:S(2)}) collective-permute-start(bf16[8,96,384]{2,1,0:T(8,128)(2,1)} %get-tuple-element.93), channel_id=1, source_target_pairs={{0,1},{1,0},{2,3},{3,2},{4,5},{5,4},{6,7},{7,6},{8,9},{9,8},{10,11... | collective-permute-start | bytes 1769480 | tf_op jit(solution)/shard_map/ppermute | solution.py:739
  158.4 58.3 %collective-permute-start.15 = (bf16[8,96,384]{2,1,0:T(8,128)(2,1)}, bf16[8,96,384]{2,1,0:T(8,128)(2,1)}, u32[]{:S(2)}, u32[]{:S(2)}) collective-permute-start(bf16[8,96,384]{2,1,0:T(8,128)(2,1)} %get-tuple-element.94), channel_id=1, source_target_pairs={{0,2},{1,3},{2,0},{3,1},{4,6},{5,7},{6,4},{7,5},{8,10},{9,11},{10,... | collective-permute-start | bytes 1769480 | tf_op jit(solution)/shard_map/ppermute | solution.py:739
  158.4 58.3 %collective-permute-start.16 = (bf16[8,96,384]{2,1,0:T(8,128)(2,1)S(1)}, bf16[8,96,384]{2,1,0:T(8,128)(2,1)}, u32[]{:S(2)}, u32[]{:S(2)}) collective-permute-start(bf16[8,96,384]{2,1,0:T(8,128)(2,1)S(1)} %copy-done.51), channel_id=1, source_target_pairs={{0,3},{1,2},{2,1},{3,0},{4,7},{5,6},{6,5},{7,4},{8,11},{9,10},{10,... | collective-permute-start | bytes 1769480 | tf_op jit(solution)/shard_map/ppermute | solution.py:739
  161.7 56.6 %collective-permute-start.17 = (bf16[8,96,384]{2,1,0:T(8,128)(2,1)S(1)}, bf16[8,96,384]{2,1,0:T(8,128)(2,1)}, u32[]{:S(2)}, u32[]{:S(2)}) collective-permute-start(bf16[8,96,384]{2,1,0:T(8,128)(2,1)S(1)} %copy-done.49), channel_id=1, source_target_pairs={{0,4},{1,5},{2,6},{3,7},{4,0},{5,1},{6,2},{7,3},{8,12},{9,13},{10,... | collective-permute-start | bytes 1769480 | tf_op jit(solution)/shard_map/ppermute | solution.py:739
  213.4 53.9 %collective-permute-start.18 = (bf16[8,96,384]{2,1,0:T(8,128)(2,1)S(1)}, bf16[8,96,384]{2,1,0:T(8,128)(2,1)}, u32[]{:S(2)}, u32[]{:S(2)}) collective-permute-start(bf16[8,96,384]{2,1,0:T(8,128)(2,1)S(1)} %copy-done.38), channel_id=1, source_target_pairs={{0,5},{1,4},{2,7},{3,6},{4,1},{5,0},{6,3},{7,2},{8,13},{9,12},{10,... | collective-permute-start | bytes 1769480 | tf_op jit(solution)/shard_map/ppermute | solution.py:739
  215.1 52.7 %collective-permute-start.19 = (bf16[8,96,384]{2,1,0:T(8,128)(2,1)S(1)}, bf16[8,96,384]{2,1,0:T(8,128)(2,1)}, u32[]{:S(2)}, u32[]{:S(2)}) collective-permute-start(bf16[8,96,384]{2,1,0:T(8,128)(2,1)S(1)} %copy-done.36), channel_id=1, source_target_pairs={{0,6},{1,7},{2,4},{3,5},{4,2},{5,3},{6,0},{7,1},{8,14},{9,15},{10,... | collective-permute-start | bytes 1769480 | tf_op jit(solution)/shard_map/ppermute | solution.py:739
  216.7 52.5 %collective-permute-start.20 = (bf16[8,96,384]{2,1,0:T(8,128)(2,1)S(1)}, bf16[8,96,384]{2,1,0:T(8,128)(2,1)}, u32[]{:S(2)}, u32[]{:S(2)}) collective-permute-start(bf16[8,96,384]{2,1,0:T(8,128)(2,1)S(1)} %copy-done.34), channel_id=1, source_target_pairs={{0,7},{1,6},{2,5},{3,4},{4,3},{5,2},{6,1},{7,0},{8,15},{9,14},{10,... | collective-permute-start | bytes 1769480 | tf_op jit(solution)/shard_map/ppermute | solution.py:739
  216.8 54.0 %collective-permute-start = (bf16[8,96,384]{2,1,0:T(8,128)(2,1)}, bf16[8,96,384]{2,1,0:T(8,128)(2,1)S(1)}, u32[]{:S(2)}, u32[]{:S(2)}) collective-permute-start(bf16[8,96,384]{2,1,0:T(8,128)(2,1)} %get-tuple-element.77), channel_id=1, source_target_pairs={{0,1},{1,0},{2,3},{3,2},{4,5},{5,4},{6,7},{7,6},{8,9},{9,8},{10,11... | collective-permute-start | bytes 1769480 | tf_op jit(solution)/shard_map/ppermute | solution.py:739
  218.3 53.3 %collective-permute-start.1 = (bf16[8,96,384]{2,1,0:T(8,128)(2,1)S(1)}, bf16[8,96,384]{2,1,0:T(8,128)(2,1)}, u32[]{:S(2)}, u32[]{:S(2)}) collective-permute-start(bf16[8,96,384]{2,1,0:T(8,128)(2,1)S(1)} %copy-done.54), channel_id=1, source_target_pairs={{0,2},{1,3},{2,0},{3,1},{4,6},{5,7},{6,4},{7,5},{8,10},{9,11},{10,... | collective-permute-start | bytes 1769480 | tf_op jit(solution)/shard_map/ppermute | solution.py:739
  267.3 53.4 %collective-permute-start.2 = (bf16[8,96,384]{2,1,0:T(8,128)(2,1)S(1)}, bf16[8,96,384]{2,1,0:T(8,128)(2,1)S(1)}, u32[]{:S(2)}, u32[]{:S(2)}) collective-permute-start(bf16[8,96,384]{2,1,0:T(8,128)(2,1)S(1)} %copy-done.47), channel_id=1, source_target_pairs={{0,3},{1,2},{2,1},{3,0},{4,7},{5,6},{6,5},{7,4},{8,11},{9,10},{10,... | collective-permute-start | bytes 1769480 | tf_op jit(solution)/shard_map/ppermute | solution.py:739
  267.8 52.9 %collective-permute-start.3 = (bf16[8,96,384]{2,1,0:T(8,128)(2,1)S(1)}, bf16[8,96,384]{2,1,0:T(8,128)(2,1)S(1)}, u32[]{:S(2)}, u32[]{:S(2)}) collective-permute-start(bf16[8,96,384]{2,1,0:T(8,128)(2,1)S(1)} %copy-done.46), channel_id=1, source_target_pairs={{0,4},{1,5},{2,6},{3,7},{4,0},{5,1},{6,2},{7,3},{8,12},{9,13},{10,... | collective-permute-start | bytes 1769480 | tf_op jit(solution)/shard_map/ppermute | solution.py:739
  269.2 51.6 %collective-permute-start.4 = (bf16[8,96,384]{2,1,0:T(8,128)(2,1)S(1)}, bf16[8,96,384]{2,1,0:T(8,128)(2,1)S(1)}, u32[]{:S(2)}, u32[]{:S(2)}) collective-permute-start(bf16[8,96,384]{2,1,0:T(8,128)(2,1)S(1)} %copy-done.44), channel_id=1, source_target_pairs={{0,5},{1,4},{2,7},{3,6},{4,1},{5,0},{6,3},{7,2},{8,13},{9,12},{10,... | collective-permute-start | bytes 1769480 | tf_op jit(solution)/shard_map/ppermute | solution.py:739
  270.8 50.0 %collective-permute-start.5 = (bf16[8,96,384]{2,1,0:T(8,128)(2,1)S(1)}, bf16[8,96,384]{2,1,0:T(8,128)(2,1)}, u32[]{:S(2)}, u32[]{:S(2)}) collective-permute-start(bf16[8,96,384]{2,1,0:T(8,128)(2,1)S(1)} %copy-done.43), channel_id=1, source_target_pairs={{0,6},{1,7},{2,4},{3,5},{4,2},{5,3},{6,0},{7,1},{8,14},{9,15},{10,... | collective-permute-start | bytes 1769480 | tf_op jit(solution)/shard_map/ppermute | solution.py:739
  271.6 49.8 %collective-permute-start.6 = (bf16[8,96,384]{2,1,0:T(8,128)(2,1)S(1)}, bf16[8,96,384]{2,1,0:T(8,128)(2,1)S(1)}, u32[]{:S(2)}, u32[]{:S(2)}) collective-permute-start(bf16[8,96,384]{2,1,0:T(8,128)(2,1)S(1)} %copy-done.42), channel_id=1, source_target_pairs={{0,7},{1,6},{2,5},{3,4},{4,3},{5,2},{6,1},{7,0},{8,15},{9,14},{10,... | collective-permute-start | bytes 1769480 | tf_op jit(solution)/shard_map/ppermute | solution.py:739
  375.0 40.7 %collective-permute-start.51 = (bf16[8,96,256]{2,1,0:T(8,128)(2,1)S(1)}, bf16[8,96,256]{2,1,0:T(8,128)(2,1)S(1)}, u32[]{:S(2)}, u32[]{:S(2)}) collective-permute-start(bf16[8,96,256]{2,1,0:T(8,128)(2,1)S(1)} %copy-done.72), channel_id=1, source_target_pairs={{0,3},{1,2},{2,1},{3,0},{4,7},{5,6},{6,5},{7,4},{8,11},{9,10},{10,... | collective-permute-start | bytes 1179656 | tf_op jit(solution)/shard_map/ppermute | solution.py:739
  488.8 39.8 %collective-permute-start.11 = (bf16[8,96,256]{2,1,0:T(8,128)(2,1)S(1)}, bf16[8,96,256]{2,1,0:T(8,128)(2,1)S(1)}, u32[]{:S(2)}, u32[]{:S(2)}) collective-permute-start(bf16[8,96,256]{2,1,0:T(8,128)(2,1)S(1)} %copy-done.71), channel_id=1, source_target_pairs={{0,5},{1,4},{2,7},{3,6},{4,1},{5,0},{6,3},{7,2},{8,13},{9,12},{10,... | collective-permute-start | bytes 1179656 | tf_op jit(solution)/shard_map/ppermute | solution.py:739
  494.8 42.4 %collective-permute-start.12 = (bf16[8,96,256]{2,1,0:T(8,128)(2,1)}, bf16[8,96,256]{2,1,0:T(8,128)(2,1)}, u32[]{:S(2)}, u32[]{:S(2)}) collective-permute-start(bf16[8,96,256]{2,1,0:T(8,128)(2,1)} %get-tuple-element.90), channel_id=1, source_target_pairs={{0,6},{1,7},{2,4},{3,5},{4,2},{5,3},{6,0},{7,1},{8,14},{9,15},{10,... | collective-permute-start | bytes 1179656 | tf_op jit(solution)/shard_map/ppermute | solution.py:739
  503.3 42.9 %collective-permute-start.13 = (bf16[8,96,256]{2,1,0:T(8,128)(2,1)}, bf16[8,96,256]{2,1,0:T(8,128)(2,1)}, u32[]{:S(2)}, u32[]{:S(2)}) collective-permute-start(bf16[8,96,256]{2,1,0:T(8,128)(2,1)} %get-tuple-element.91), channel_id=1, source_target_pairs={{0,7},{1,6},{2,5},{3,4},{4,3},{5,2},{6,1},{7,0},{8,15},{9,14},{10,... | collective-permute-start | bytes 1179656 | tf_op jit(solution)/shard_map/ppermute | solution.py:739
  (117 other events, 5103.4 us)

commit v3 on v2

--- a/solution.py
+++ b/solution.py
@@ -21,6 +21,11 @@
 OUT_SLOTS = ("uy", "uz", "ux", "wy", "wz", "fx", "fy", "fz")
 MAX_CHUNKS = 4
 PAIRS = 2
+WAVE_UNROLL = 4
+MOVE_UNROLL = 1
+LAST_UNROLL = 2
+SPEC_UNROLL = 1
+PLANE_UNROLL = 2
 HID_BLOCKS = 1
 UNROLL = 4
 BACK_SLOTS = ("ax", "az", "gy", "gz", "ay")
@@ -109,7 +114,7 @@
                 out_ref[k, slot, :, lanes] = value.astype(BF16)
         return carry
 
-    lax.fori_loop(0, block, one, 0)
+    lax.fori_loop(0, block, one, 0, unroll=SPEC_UNROLL)
 
 
 def make_spectra(ky, kz_col, state, cotangent):
@@ -158,7 +163,7 @@
                 scratch[v, pl.ds(start, rows), pl.ds(0, live - v * LANES)] = value[:, v * LANES :]
         return carry
 
-    lax.fori_loop(0, block, one, 0)
+    lax.fori_loop(0, block, one, 0, unroll=WAVE_UNROLL)
 
     @pl.when(step == pl.num_programs(0) - 1)
     def _():
@@ -173,7 +178,7 @@
                     out_ref[x, :, pl.ds(v * LANES, LANES)] = block_rows
             return carry
 
-        lax.fori_loop(0, span, move, 0)
+        lax.fori_loop(0, span, move, 0, unroll=MOVE_UNROLL)
 
 
 def along_x(partners, table, spectra, first, chunks):
@@ -298,7 +303,7 @@
             mid[py, dx, :, pl.ds(in_lanes, LANES)] = dot(ty_ref[...], extra).astype(BF16)
         return carry
 
-    lax.fori_loop(0, PATCH, section_y, 0)
+    lax.fori_loop(0, PATCH, section_y, 0, unroll=PLANE_UNROLL)
 
     def section_z(pair, carry):
         def field(name, dx):
@@ -333,7 +338,7 @@
                         target[half, parity, :, rows_here, :] = value
         return carry
 
-    lax.fori_loop(0, PATCH // 2, section_z, 0)
+    lax.fori_loop(0, PATCH // 2, section_z, 0, unroll=PLANE_UNROLL)
 
     def gather(source, at):
         per_dz = []
@@ -440,7 +445,7 @@
                 )
                 out_refs[px * parts_y + py][dx] = total.astype(BF16)
 
-    lax.fori_loop(0, PATCH // 2, section_back, 0)
+    lax.fori_loop(0, PATCH // 2, section_back, 0, unroll=PLANE_UNROLL)
 
 
 def back_groups(width_z):
@@ -556,11 +561,23 @@
 
 
 def final_kernel(
-    partner_ref, ky_ref, kz_ref, table_ref, cot_ref, *refs, steps_in, block, width_y, width_z, length
+    partner_ref,
+    ky_ref,
+    kz_ref,
+    table_ref,
+    base_ref,
+    *refs,
+    steps_in,
+    block,
+    width_y,
+    width_z,
+    length,
+    first,
 ):
     out_ref, scratch, turned = refs[-3:]
     recv_refs = refs[:-3]
     parts = partner_ref.shape[0]
+    planes = len(recv_refs) * steps_in
     step = pl.program_id(0)
     rows = 2 * width_y
     lanes = recv_refs[0].shape[2]
@@ -569,7 +586,7 @@
     def _():
         for j, recv_ref in enumerate(recv_refs):
             source = partner_ref[j % parts]
-            x = source * (length // parts) + (j // parts) * steps_in + step
+            x = (j // parts * parts + source) * steps_in + step
             at = pl.multiple_of(x * rows, 8)
             value = recv_ref[0].astype(F32)
             for v in range(lanes // LANES):
@@ -590,19 +607,19 @@
             pieces = []
             for v in range(lanes // LANES):
                 parts_s = [
-                    scratch[v, pl.ds(ky + s * width_y, length, stride=rows), :] for s in range(2)
+                    scratch[v, pl.ds(ky + s * width_y, planes, stride=rows), :] for s in range(2)
                 ]
                 pieces.append(jnp.concatenate(parts_s, axis=0))
             gathered = jnp.concatenate(pieces, axis=1).astype(BF16)
-            turned[...] = dot_tn(gathered, table_ref[...])
+            turned[k % LAST_UNROLL] = dot_tn(gathered, table_ref[...])
             wave_y = ky_ref[ky]
             kept = jnp.where(inside & (jnp.abs(wave_y) <= cutoff), 1.0, 0.0).astype(F32)
-            damped = jnp.exp(-NU_DT * (plane + wave_y * wave_y))
             scale = kept * weight
+            factor = jnp.exp(-NU_DT * (plane + wave_y * wave_y)) if first else 1.0
 
             def part(name, t):
                 at = BACK_SLOTS.index(name) * width_z
-                return turned[pl.ds(at, width_z), pl.ds(t * length, length)]
+                return turned[k % LAST_UNROLL, pl.ds(at, width_z), pl.ds(t * length, length)]
 
             for t in range(2):
                 sign = -1.0 if t == 0 else 1.0
@@ -610,14 +627,14 @@
                 ay = part("ay", t) - sign * wave_x * part("gz", 1 - t)
                 az = part("az", t) + sign * wave_x * part("gy", 1 - t)
                 for c, value in enumerate((ax, ay, az)):
-                    out_ref[c, t, k] = damped * cot_ref[c, t, k] + scale * value
+                    out_ref[c, t, k] = factor * base_ref[c, t, k] + scale * value
             return carry
 
-        lax.fori_loop(0, block, one, 0)
-
-
-def finish(partners, ky, kz_col, table, cotangent, received):
-    _, _, width_y, width_z, length = cotangent.shape
+        lax.fori_loop(0, block, one, 0, unroll=LAST_UNROLL)
+
+
+def finish(partners, ky, kz_col, table, base, received, first):
+    _, _, width_y, width_z, length = base.shape
     span, rows, lanes = received[0].shape
     block = 8
     steps_in = span
@@ -634,6 +651,7 @@
             width_y=width_y,
             width_z=width_z,
             length=length,
+            first=first,
         ),
         grid=(steps,),
         in_specs=[
@@ -645,14 +663,19 @@
         ]
         + [recv_spec] * len(received),
         out_specs=spec,
-        out_shape=jax.ShapeDtypeStruct(cotangent.shape, F32),
+        out_shape=jax.ShapeDtypeStruct(base.shape, F32),
         scratch_shapes=[
-            pltpu.VMEM((lanes // LANES, length * rows, LANES), F32),
-            pltpu.VMEM((lanes, 2 * length), F32),
+            pltpu.VMEM((lanes // LANES, len(received) * span * rows, LANES), F32),
+            pltpu.VMEM((LAST_UNROLL, lanes, 2 * length), F32),
         ],
         compiler_params=pltpu.CompilerParams(vmem_limit_bytes=60 * 2**20),
+        cost_estimate=pl.CostEstimate(
+            flops=2 * width_y * lanes * table.size * 2,
+            bytes_accessed=8 * base.size,
+            transcendentals=0,
+        ),
         name="finish",
-    )(partners, ky, kz_col, table, cotangent, *received)
+    )(partners, ky, kz_col, table, base, *received)
 
 
 def shards(state, cotangent, w_in, b_in, w_out):
@@ -684,7 +707,7 @@
     both = np.stack(
         [np.concatenate([cosine, -sine], axis=1), np.concatenate([sine, cosine], axis=1)]
     )
-    x_back = jnp.asarray(both.reshape(2 * length, 2 * length), BF16)
+    x_back = both.reshape(2, parts, chunks, span, 2 * length).transpose(2, 0, 1, 3, 4)
     x_rows = both.reshape(2, parts, chunks, span, 2 * length).transpose(1, 2, 0, 3, 4)
     x_rows = jnp.asarray(x_rows.reshape(parts, chunks, 2 * span, 2 * length), BF16)
 
@@ -758,10 +781,16 @@
         )
         returned.append(exchange(sent))
         grads = grads + jnp.concatenate([gin, gout], axis=1)
-    grads = sum(exchange([grads[k * units : (k + 1) * units] for k in range(parts)]))
-
-    received = [array for chunk in returned for array in chunk]
-    state_grad = finish(partners, ky, kz_col, x_back, cotangent, received)
+    grads = exchange([grads[k * units : (k + 1) * units] for k in range(parts)])
+    grads = sum(grads)
+
+    state_grad = cotangent
+    ends = ((0, chunks - 1), (chunks - 1, chunks)) if chunks > 1 else ((0, chunks),)
+    for j, (low, high) in enumerate(ends):
+        received = [array for chunk in returned[low:high] for array in chunk]
+        table = x_back[low:high].transpose(1, 0, 2, 3, 4).reshape(-1, 2 * length)
+        table = jnp.asarray(table, BF16)
+        state_grad = finish(partners, ky, kz_col, table, state_grad, received, j == 0)
 
     pad = up_to(feat + 1, 2 * LANES)
 

time: 605 us -> 567 us (0.937)
  Pallas kernels: 342 us -> 321 us
  waiting for transfers between devices: 169 us -> 155 us
    pallas_call x3, Pallas kernels: 81.1 us -> 64.2 us  [along_x(): pl.pallas_call(functools.partial(along_x_kernel, first=first, chunks=chun...]
    ppermute x63, waiting for transfers between devices: 169 us -> 155 us  [exchange(): moved.append(lax.ppermute(arrays[k], ('px', 'py'), pairs))]
    pallas_call x4, Pallas kernels: 194 us -> 186 us  [physical(): pl.pallas_call(functools.partial(physical_kernel, parts_x=parts_x, parts_...]
    pallas_call x1 -> x2, Pallas kernels: 48.7 us -> 52.5 us  [finish(): pl.pallas_call(functools.partial(final_kernel, steps_in=steps_in, block=b...]
  transfers between devices with their start and end apart: 63 -> 63, of which waited for: 27 -> 24; matrix products, arithmetic and copies ran while one was open for 2% -> 2% of each run, Pallas kernels for 32% -> 38%
where the time goes in v3:
time: 567 us; the launch traced here: 558 us
  Pallas kernels  321 us (57%)
  waiting for transfers between devices  155 us (27%)
  starting transfers between devices  62.2 us (11%)
  local copies, waits for them, and re-layouts  14.3 us (3%)
    pallas_call x4, Pallas kernels, physical(): pl.pallas_call(functools.partial(physical_kernel, parts_x=parts_x, parts_...  186 us
    ppermute x63, waiting for transfers between devices, exchange(): moved.append(lax.ppermute(arrays[k], ('px', 'py'), pairs))  155 us
    pallas_call x3, Pallas kernels, along_x(): pl.pallas_call(functools.partial(along_x_kernel, first=first, chunks=chun...  64.2 us
    ppermute x63, starting transfers between devices, exchange(): moved.append(lax.ppermute(arrays[k], ('px', 'py'), pairs))  62.2 us
    pallas_call x2, Pallas kernels, finish(): pl.pallas_call(functools.partial(final_kernel, steps_in=steps_in, block=b...  52.5 us
    pallas_call x1, Pallas kernels, make_spectra(): pl.pallas_call(functools.partial(spectra_kernel, block=block, length=leng...  18 us
  transfers between devices with their start and end apart: 63, of which 24 were waited for; matrix products, arithmetic and copies ran while one was open for 2% of the time, Pallas kernels for 38%

profile of v3, /device:TPU:0, one launch (start us, length us, event | category | flops | bytes accessed | tf_op | source)
XLA Modules:
  0.0 558.2 jit_solution(4294829088858706871)
XLA Ops:
  2.4 18.0 %spectra.1 = bf16[48,8,48,512]{3,2,1,0:T(8,128)(2,1)} custom-call(f32[48]{0:T(128)} %fusion.9.ky_ref, f32[48,256]{1,0:T(8,128)} %broadcast_in_dim.41.kz_ref, f32[3,2,48,48,256]{4,3,2,1,0:T(8,128)} %state_ref.1, f32[3,2,48,48,256]{4,3,2,1,0:T(8,128)} %base_ref.1), custom_call_target="tpu_custom_call" | custom-call | tf_op jit(solution)/shard_map/spectra/pallas_call | solution.py:125
  20.4 26.6 %along_x.5 = (bf16[8,96,384]{2,1,0:T(8,128)(2,1)}, bf16[8,96,384]{2,1,0:T(8,128)(2,1)}, bf16[8,96,384]{2,1,0:T(8,128)(2,1)}, bf16[8,96,384]{2,1,0:T(8,128)(2,1)}...) custom-call(s32[8]{0:T(128)} %iota_xor_fusion.1.partner_ref, ...), custom_call_target="tpu_custom_call" | custom-call | flops 9663676416 | bytes 28311552 | tf_op jit(solution)/shard_map/along_x/pallas_call | solution.py:192
  55.6 9.0 %collective-permute-done.42.refs_1_ = bf16[8,96,384]{2,1,0:T(8,128)(2,1)S(1)} collective-permute-done((bf16[8,96,384]{2,1,0:T(8,128)(2,1)}, bf16[8,96,384]{2,1,0:T(8,128)(2,1)S(1)}, u32[]{:S(2)}, u32[]{:S(2)}) %collective-permute-start.42) | collective-permute-done | bytes 589856 | tf_op jit(solution)/shard_map/ppermute | solution.py:762
  67.7 20.6 %collective-permute-done.44.refs_3_ = bf16[8,96,384]{2,1,0:T(8,128)(2,1)S(1)} collective-permute-done((bf16[8,96,384]{2,1,0:T(8,128)(2,1)}, bf16[8,96,384]{2,1,0:T(8,128)(2,1)S(1)}, u32[]{:S(2)}, u32[]{:S(2)}) %collective-permute-start.44) | collective-permute-done | bytes 589856 | tf_op jit(solution)/shard_map/ppermute | solution.py:762
  90.5 18.8 %along_x.4 = (bf16[8,96,384]{2,1,0:T(8,128)(2,1)}, bf16[8,96,384]{2,1,0:T(8,128)(2,1)}, bf16[8,96,384]{2,1,0:T(8,128)(2,1)}, bf16[8,96,384]{2,1,0:T(8,128)(2,1)}...) custom-call(s32[8]{0:T(128)} %iota_xor_fusion.1.partner_ref, ...), custom_call_target="tpu_custom_call" | custom-call | flops 4831838208 | bytes 23592960 | tf_op jit(solution)/shard_map/along_x/pallas_call | solution.py:192
  125.7 18.7 %along_x.3 = (bf16[8,96,384]{2,1,0:T(8,128)(2,1)}, bf16[8,96,384]{2,1,0:T(8,128)(2,1)}, bf16[8,96,384]{2,1,0:T(8,128)(2,1)}, bf16[8,96,384]{2,1,0:T(8,128)(2,1)}...) custom-call(s32[8]{0:T(128)} %iota_xor_fusion.1.partner_ref, ...), custom_call_target="tpu_custom_call" | custom-call | flops 4831838208 | bytes 23592960 | tf_op jit(solution)/shard_map/along_x/pallas_call | solution.py:192
  154.3 46.5 %physical.7 = (bf16[8,96,256]{2,1,0:T(8,128)(2,1)}, bf16[8,96,256]{2,1,0:T(8,128)(2,1)}, bf16[8,96,256]{2,1,0:T(8,128)(2,1)}, bf16[8,96,256]{2,1,0:T(8,128)(2,1)...) custom-call(bf16[8,96,384]{2,1,0:T(8,128)(2,1)} %get-tuple-element.1, ...), custom_call_target="tpu_custom_call" | custom-call | flops 21474836480 | bytes 9437184 | tf_op jit(solution)/shard_map/physical/pallas_call | solution.py:523
  206.2 46.6 %physical.6 = (bf16[8,96,256]{2,1,0:T(8,128)(2,1)}, bf16[8,96,256]{2,1,0:T(8,128)(2,1)}, bf16[8,96,256]{2,1,0:T(8,128)(2,1)}, bf16[8,96,256]{2,1,0:T(8,128)(2,1)...) custom-call(bf16[8,96,384]{2,1,0:T(8,128)(2,1)} %get-tuple-element.1, ...), custom_call_target="tpu_custom_call" | custom-call | flops 21474836480 | bytes 9437184 | tf_op jit(solution)/shard_map/physical/pallas_call | solution.py:523
  258.1 46.2 %physical.5 = (bf16[8,96,256]{2,1,0:T(8,128)(2,1)}, bf16[8,96,256]{2,1,0:T(8,128)(2,1)}, bf16[8,96,256]{2,1,0:T(8,128)(2,1)}, bf16[8,96,256]{2,1,0:T(8,128)(2,1)...) custom-call(bf16[8,96,384]{2,1,0:T(8,128)(2,1)} %get-tuple-element.9, ...), custom_call_target="tpu_custom_call" | custom-call | flops 21474836480 | bytes 9437184 | tf_op jit(solution)/shard_map/physical/pallas_call | solution.py:523
  307.1 46.6 %physical.4 = (bf16[8,96,256]{2,1,0:T(8,128)(2,1)}, bf16[8,96,256]{2,1,0:T(8,128)(2,1)}, bf16[8,96,256]{2,1,0:T(8,128)(2,1)}, bf16[8,96,256]{2,1,0:T(8,128)(2,1)...) custom-call(bf16[8,96,384]{2,1,0:T(8,128)(2,1)} %get-tuple-element.7, ...), custom_call_target="tpu_custom_call" | custom-call | flops 21474836480 | bytes 9437184 | tf_op jit(solution)/shard_map/physical/pallas_call | solution.py:523
  363.5 17.2 %collective-permute-done.58 = f32[64,448]{1,0:T(8,128)S(1)} collective-permute-done((f32[64,448]{1,0:T(8,128)S(1)}, f32[64,448]{1,0:T(8,128)S(1)}, u32[]{:S(2)}, u32[]{:S(2)}) %collective-permute-start.58) | collective-permute-done | bytes 114720 | tf_op jit(solution)/shard_map/ppermute | solution.py:762
  382.1 5.8 %collective-permute-done.60 = f32[64,448]{1,0:T(8,128)S(1)} collective-permute-done((f32[64,448]{1,0:T(8,128)S(1)}, f32[64,448]{1,0:T(8,128)S(1)}, u32[]{:S(2)}, u32[]{:S(2)}) %collective-permute-start.60) | collective-permute-done | bytes 114720 | tf_op jit(solution)/shard_map/ppermute | solution.py:762
  399.4 5.7 %collective-permute-done.37.refs_19_ = bf16[8,96,256]{2,1,0:T(8,128)(2,1)S(1)} collective-permute-done((bf16[8,96,256]{2,1,0:T(8,128)(2,1)}, bf16[8,96,256]{2,1,0:T(8,128)(2,1)S(1)}, u32[]{:S(2)}, u32[]{:S(2)}) %collective-permute-start.37) | collective-permute-done | bytes 393248 | tf_op jit(solution)/shard_map/ppermute | solution.py:762
  407.0 8.3 %collective-permute-done.39.refs_21_ = bf16[8,96,256]{2,1,0:T(8,128)(2,1)S(1)} collective-permute-done((bf16[8,96,256]{2,1,0:T(8,128)(2,1)}, bf16[8,96,256]{2,1,0:T(8,128)(2,1)S(1)}, u32[]{:S(2)}, u32[]{:S(2)}) %collective-permute-start.39) | collective-permute-done | bytes 393248 | tf_op jit(solution)/shard_map/ppermute | solution.py:762
  415.6 7.2 %collective-permute-done.40.refs_22_ = bf16[8,96,256]{2,1,0:T(8,128)(2,1)S(1)} collective-permute-done((bf16[8,96,256]{2,1,0:T(8,128)(2,1)}, bf16[8,96,256]{2,1,0:T(8,128)(2,1)S(1)}, u32[]{:S(2)}, u32[]{:S(2)}) %collective-permute-start.40) | collective-permute-done | bytes 393248 | tf_op jit(solution)/shard_map/ppermute | solution.py:762
  423.7 7.7 %collective-permute-done.41.refs_23_ = bf16[8,96,256]{2,1,0:T(8,128)(2,1)S(1)} collective-permute-done((bf16[8,96,256]{2,1,0:T(8,128)(2,1)}, bf16[8,96,256]{2,1,0:T(8,128)(2,1)S(1)}, u32[]{:S(2)}, u32[]{:S(2)}) %collective-permute-start.41) | collective-permute-done | bytes 393248 | tf_op jit(solution)/shard_map/ppermute | solution.py:762
  443.4 5.6 %collective-permute-done.25.refs_13_ = bf16[8,96,256]{2,1,0:T(8,128)(2,1)S(1)} collective-permute-done((bf16[8,96,256]{2,1,0:T(8,128)(2,1)}, bf16[8,96,256]{2,1,0:T(8,128)(2,1)S(1)}, u32[]{:S(2)}, u32[]{:S(2)}) %collective-permute-start.25) | collective-permute-done | bytes 393248 | tf_op jit(solution)/shard_map/ppermute | solution.py:762
  449.5 7.0 %collective-permute-done.26.refs_14_ = bf16[8,96,256]{2,1,0:T(8,128)(2,1)S(1)} collective-permute-done((bf16[8,96,256]{2,1,0:T(8,128)(2,1)}, bf16[8,96,256]{2,1,0:T(8,128)(2,1)S(1)}, u32[]{:S(2)}, u32[]{:S(2)}) %collective-permute-start.26) | collective-permute-done | bytes 393248 | tf_op jit(solution)/shard_map/ppermute | solution.py:762
  457.6 7.4 %collective-permute-done.27.refs_15_ = bf16[8,96,256]{2,1,0:T(8,128)(2,1)S(1)} collective-permute-done((bf16[8,96,256]{2,1,0:T(8,128)(2,1)}, bf16[8,96,256]{2,1,0:T(8,128)(2,1)S(1)}, u32[]{:S(2)}, u32[]{:S(2)}) %collective-permute-start.27) | collective-permute-done | bytes 393248 | tf_op jit(solution)/shard_map/ppermute | solution.py:762
  466.5 8.0 %collective-permute-done.10.refs_4_ = bf16[8,96,256]{2,1,0:T(8,128)(2,1)S(1)} collective-permute-done((bf16[8,96,256]{2,1,0:T(8,128)(2,1)}, bf16[8,96,256]{2,1,0:T(8,128)(2,1)S(1)}, u32[]{:S(2)}, u32[]{:S(2)}) %collective-permute-start.10) | collective-permute-done | bytes 393248 | tf_op jit(solution)/shard_map/ppermute | solution.py:762
  474.5 8.3 %collective-permute-done.11.refs_5_ = bf16[8,96,256]{2,1,0:T(8,128)(2,1)S(1)} collective-permute-done((bf16[8,96,256]{2,1,0:T(8,128)(2,1)}, bf16[8,96,256]{2,1,0:T(8,128)(2,1)S(1)}, u32[]{:S(2)}, u32[]{:S(2)}) %collective-permute-start.11) | collective-permute-done | bytes 393248 | tf_op jit(solution)/shard_map/ppermute | solution.py:762
  491.6 7.4 %collective-permute-done.13.refs_7_ = bf16[8,96,256]{2,1,0:T(8,128)(2,1)} collective-permute-done((bf16[8,96,256]{2,1,0:T(8,128)(2,1)}, bf16[8,96,256]{2,1,0:T(8,128)(2,1)}, u32[]{:S(2)}, u32[]{:S(2)}) %collective-permute-start.13) | collective-permute-done | bytes 393248 | tf_op jit(solution)/shard_map/ppermute | solution.py:762
  504.4 33.2 %finish.2.base_ref = f32[3,2,48,48,256]{4,3,2,1,0:T(8,128)} custom-call(s32[8]{0:T(128)} %iota_xor_fusion.1.partner_ref, f32[48]{0:T(128)} %fusion.9.ky_ref, f32[48,256]{1,0:T(8,128)} %broadcast_in_dim.41.kz_ref, bf16[384,512]{1,0:T(8,128)(2,1)} %constant.88.clone.table_ref, f32[3,2,48,48,256]{4,3,2,1,0:T(8,128)} %base_ref.1, ...), custom_call_target="tpu_custom_call" | custom-call | flops 9663676416 | bytes 28311552 | tf_op jit(solution)/shard_map/finish/pallas_call | solution.py:646
  538.4 19.3 %finish.3 = f32[3,2,48,48,256]{4,3,2,1,0:T(8,128)} custom-call(s32[8]{0:T(128)} %iota_xor_fusion.1.partner_ref, f32[48]{0:T(128)} %fusion.9.ky_ref, f32[48,256]{1,0:T(8,128)} %broadcast_in_dim.41.kz_ref, bf16[128,512]{1,0:T(8,128)(2,1)} %constant.89.clone.table_ref, f32[3,2,48,48,256]{4,3,2,1,0:T(8,128)} %finish.2.base_ref, ...), custom_call_target="tpu_custom_call" | custom-call | flops 3221225472 | bytes 28311552 | tf_op jit(solution)/shard_map/finish/pallas_call | solution.py:646
  (277 shorter events, 110.4 us)
Async XLA Ops:
  50.3 58.9 %collective-permute-start.45 = (bf16[8,96,384]{2,1,0:T(8,128)(2,1)}, bf16[8,96,384]{2,1,0:T(8,128)(2,1)}, u32[]{:S(2)}, u32[]{:S(2)}) collective-permute-start(bf16[8,96,384]{2,1,0:T(8,128)(2,1)} %get-tuple-element.128), channel_id=1, source_target_pairs={{0,4},{1,5},{2,6},{3,7},{4,0},{5,1},{6,2},{7,3},{8,12},{9,13},{10,... | collective-permute-start | bytes 1769480 | tf_op jit(solution)/shard_map/ppermute | solution.py:762
  52.2 58.0 %collective-permute-start.46 = (bf16[8,96,384]{2,1,0:T(8,128)(2,1)}, bf16[8,96,384]{2,1,0:T(8,128)(2,1)}, u32[]{:S(2)}, u32[]{:S(2)}) collective-permute-start(bf16[8,96,384]{2,1,0:T(8,128)(2,1)} %get-tuple-element.129), channel_id=1, source_target_pairs={{0,5},{1,4},{2,7},{3,6},{4,1},{5,0},{6,3},{7,2},{8,13},{9,12},{10,... | collective-permute-start | bytes 1769480 | tf_op jit(solution)/shard_map/ppermute | solution.py:762
  64.5 45.7 %collective-permute-start.47 = (bf16[8,96,384]{2,1,0:T(8,128)(2,1)}, bf16[8,96,384]{2,1,0:T(8,128)(2,1)S(1)}, u32[]{:S(2)}, u32[]{:S(2)}) collective-permute-start(bf16[8,96,384]{2,1,0:T(8,128)(2,1)} %get-tuple-element.130), channel_id=1, source_target_pairs={{0,6},{1,7},{2,4},{3,5},{4,2},{5,3},{6,0},{7,1},{8,14},{9,15},{10,... | collective-permute-start | bytes 1769480 | tf_op jit(solution)/shard_map/ppermute | solution.py:762
  64.5 47.4 %collective-permute-start.48 = (bf16[8,96,384]{2,1,0:T(8,128)(2,1)}, bf16[8,96,384]{2,1,0:T(8,128)(2,1)S(1)}, u32[]{:S(2)}, u32[]{:S(2)}) collective-permute-start(bf16[8,96,384]{2,1,0:T(8,128)(2,1)} %get-tuple-element.131), channel_id=1, source_target_pairs={{0,7},{1,6},{2,5},{3,4},{4,3},{5,2},{6,1},{7,0},{8,15},{9,14},{10,... | collective-permute-start | bytes 1769480 | tf_op jit(solution)/shard_map/ppermute | solution.py:762
  144.5 56.3 %collective-permute-start.34 = (bf16[8,96,384]{2,1,0:T(8,128)(2,1)S(1)}, bf16[8,96,384]{2,1,0:T(8,128)(2,1)}, u32[]{:S(2)}, u32[]{:S(2)}) collective-permute-start(bf16[8,96,384]{2,1,0:T(8,128)(2,1)S(1)} %copy-done.31), channel_id=1, source_target_pairs={{0,7},{1,6},{2,5},{3,4},{4,3},{5,2},{6,1},{7,0},{8,15},{9,14},{10,... | collective-permute-start | bytes 1769480 | tf_op jit(solution)/shard_map/ppermute | solution.py:762
  145.1 57.4 %collective-permute-start.14 = (bf16[8,96,384]{2,1,0:T(8,128)(2,1)S(1)}, bf16[8,96,384]{2,1,0:T(8,128)(2,1)S(1)}, u32[]{:S(2)}, u32[]{:S(2)}) collective-permute-start(bf16[8,96,384]{2,1,0:T(8,128)(2,1)S(1)} %copy-done.48), channel_id=1, source_target_pairs={{0,1},{1,0},{2,3},{3,2},{4,5},{5,4},{6,7},{7,6},{8,9},{9,8},{10,11... | collective-permute-start | bytes 1769480 | tf_op jit(solution)/shard_map/ppermute | solution.py:762
  146.5 57.7 %collective-permute-start.15 = (bf16[8,96,384]{2,1,0:T(8,128)(2,1)S(1)}, bf16[8,96,384]{2,1,0:T(8,128)(2,1)S(1)}, u32[]{:S(2)}, u32[]{:S(2)}) collective-permute-start(bf16[8,96,384]{2,1,0:T(8,128)(2,1)S(1)} %copy-done.46), channel_id=1, source_target_pairs={{0,2},{1,3},{2,0},{3,1},{4,6},{5,7},{6,4},{7,5},{8,10},{9,11},{10,... | collective-permute-start | bytes 1769480 | tf_op jit(solution)/shard_map/ppermute | solution.py:762
  146.5 57.8 %collective-permute-start.16 = (bf16[8,96,384]{2,1,0:T(8,128)(2,1)S(1)}, bf16[8,96,384]{2,1,0:T(8,128)(2,1)}, u32[]{:S(2)}, u32[]{:S(2)}) collective-permute-start(bf16[8,96,384]{2,1,0:T(8,128)(2,1)S(1)} %copy-done.44), channel_id=1, source_target_pairs={{0,3},{1,2},{2,1},{3,0},{4,7},{5,6},{6,5},{7,4},{8,11},{9,10},{10,... | collective-permute-start | bytes 1769480 | tf_op jit(solution)/shard_map/ppermute | solution.py:762
  151.3 54.6 %collective-permute-start.17 = (bf16[8,96,384]{2,1,0:T(8,128)(2,1)S(1)}, bf16[8,96,384]{2,1,0:T(8,128)(2,1)}, u32[]{:S(2)}, u32[]{:S(2)}) collective-permute-start(bf16[8,96,384]{2,1,0:T(8,128)(2,1)S(1)} %copy-done.43), channel_id=1, source_target_pairs={{0,4},{1,5},{2,6},{3,7},{4,0},{5,1},{6,2},{7,3},{8,12},{9,13},{10,... | collective-permute-start | bytes 1769480 | tf_op jit(solution)/shard_map/ppermute | solution.py:762
  200.8 52.0 %collective-permute-start.18 = (bf16[8,96,384]{2,1,0:T(8,128)(2,1)S(1)}, bf16[8,96,384]{2,1,0:T(8,128)(2,1)}, u32[]{:S(2)}, u32[]{:S(2)}) collective-permute-start(bf16[8,96,384]{2,1,0:T(8,128)(2,1)S(1)} %copy-done.34), channel_id=1, source_target_pairs={{0,5},{1,4},{2,7},{3,6},{4,1},{5,0},{6,3},{7,2},{8,13},{9,12},{10,... | collective-permute-start | bytes 1769480 | tf_op jit(solution)/shard_map/ppermute | solution.py:762
  202.5 50.8 %collective-permute-start.19 = (bf16[8,96,384]{2,1,0:T(8,128)(2,1)S(1)}, bf16[8,96,384]{2,1,0:T(8,128)(2,1)}, u32[]{:S(2)}, u32[]{:S(2)}) collective-permute-start(bf16[8,96,384]{2,1,0:T(8,128)(2,1)S(1)} %copy-done.32), channel_id=1, source_target_pairs={{0,6},{1,7},{2,4},{3,5},{4,2},{5,3},{6,0},{7,1},{8,14},{9,15},{10,... | collective-permute-start | bytes 1769480 | tf_op jit(solution)/shard_map/ppermute | solution.py:762
  204.2 50.4 %collective-permute-start.20 = (bf16[8,96,384]{2,1,0:T(8,128)(2,1)S(1)}, bf16[8,96,384]{2,1,0:T(8,128)(2,1)}, u32[]{:S(2)}, u32[]{:S(2)}) collective-permute-start(bf16[8,96,384]{2,1,0:T(8,128)(2,1)S(1)} %copy-done.30), channel_id=1, source_target_pairs={{0,7},{1,6},{2,5},{3,4},{4,3},{5,2},{6,1},{7,0},{8,15},{9,14},{10,... | collective-permute-start | bytes 1769480 | tf_op jit(solution)/shard_map/ppermute | solution.py:762
  204.3 51.9 %collective-permute-start = (bf16[8,96,384]{2,1,0:T(8,128)(2,1)}, bf16[8,96,384]{2,1,0:T(8,128)(2,1)S(1)}, u32[]{:S(2)}, u32[]{:S(2)}) collective-permute-start(bf16[8,96,384]{2,1,0:T(8,128)(2,1)} %get-tuple-element.77), channel_id=1, source_target_pairs={{0,1},{1,0},{2,3},{3,2},{4,5},{5,4},{6,7},{7,6},{8,9},{9,8},{10,11... | collective-permute-start | bytes 1769480 | tf_op jit(solution)/shard_map/ppermute | solution.py:762
  205.8 51.3 %collective-permute-start.1 = (bf16[8,96,384]{2,1,0:T(8,128)(2,1)}, bf16[8,96,384]{2,1,0:T(8,128)(2,1)S(1)}, u32[]{:S(2)}, u32[]{:S(2)}) collective-permute-start(bf16[8,96,384]{2,1,0:T(8,128)(2,1)} %get-tuple-element.78), channel_id=1, source_target_pairs={{0,2},{1,3},{2,0},{3,1},{4,6},{5,7},{6,4},{7,5},{8,10},{9,11},{10,... | collective-permute-start | bytes 1769480 | tf_op jit(solution)/shard_map/ppermute | solution.py:762
  252.8 51.5 %collective-permute-start.2 = (bf16[8,96,384]{2,1,0:T(8,128)(2,1)S(1)}, bf16[8,96,384]{2,1,0:T(8,128)(2,1)S(1)}, u32[]{:S(2)}, u32[]{:S(2)}) collective-permute-start(bf16[8,96,384]{2,1,0:T(8,128)(2,1)S(1)} %copy-done.42), channel_id=1, source_target_pairs={{0,3},{1,2},{2,1},{3,0},{4,7},{5,6},{6,5},{7,4},{8,11},{9,10},{10,... | collective-permute-start | bytes 1769480 | tf_op jit(solution)/shard_map/ppermute | solution.py:762
  253.3 51.0 %collective-permute-start.3 = (bf16[8,96,384]{2,1,0:T(8,128)(2,1)S(1)}, bf16[8,96,384]{2,1,0:T(8,128)(2,1)S(1)}, u32[]{:S(2)}, u32[]{:S(2)}) collective-permute-start(bf16[8,96,384]{2,1,0:T(8,128)(2,1)S(1)} %copy-done.41), channel_id=1, source_target_pairs={{0,4},{1,5},{2,6},{3,7},{4,0},{5,1},{6,2},{7,3},{8,12},{9,13},{10,... | collective-permute-start | bytes 1769480 | tf_op jit(solution)/shard_map/ppermute | solution.py:762
  254.6 49.7 %collective-permute-start.4 = (bf16[8,96,384]{2,1,0:T(8,128)(2,1)S(1)}, bf16[8,96,384]{2,1,0:T(8,128)(2,1)S(1)}, u32[]{:S(2)}, u32[]{:S(2)}) collective-permute-start(bf16[8,96,384]{2,1,0:T(8,128)(2,1)S(1)} %copy-done.40), channel_id=1, source_target_pairs={{0,5},{1,4},{2,7},{3,6},{4,1},{5,0},{6,3},{7,2},{8,13},{9,12},{10,... | collective-permute-start | bytes 1769480 | tf_op jit(solution)/shard_map/ppermute | solution.py:762
  256.2 48.1 %collective-permute-start.5 = (bf16[8,96,384]{2,1,0:T(8,128)(2,1)S(1)}, bf16[8,96,384]{2,1,0:T(8,128)(2,1)}, u32[]{:S(2)}, u32[]{:S(2)}) collective-permute-start(bf16[8,96,384]{2,1,0:T(8,128)(2,1)S(1)} %copy-done.39), channel_id=1, source_target_pairs={{0,6},{1,7},{2,4},{3,5},{4,2},{5,3},{6,0},{7,1},{8,14},{9,15},{10,... | collective-permute-start | bytes 1769480 | tf_op jit(solution)/shard_map/ppermute | solution.py:762
  257.1 49.9 %collective-permute-start.6 = (bf16[8,96,384]{2,1,0:T(8,128)(2,1)S(1)}, bf16[8,96,384]{2,1,0:T(8,128)(2,1)}, u32[]{:S(2)}, u32[]{:S(2)}) collective-permute-start(bf16[8,96,384]{2,1,0:T(8,128)(2,1)S(1)} %copy-done.38), channel_id=1, source_target_pairs={{0,7},{1,6},{2,5},{3,4},{4,3},{5,2},{6,1},{7,0},{8,15},{9,14},{10,... | collective-permute-start | bytes 1769480 | tf_op jit(solution)/shard_map/ppermute | solution.py:762
  357.5 39.1 %collective-permute-start.35 = (bf16[8,96,256]{2,1,0:T(8,128)(2,1)S(1)}, bf16[8,96,256]{2,1,0:T(8,128)(2,1)S(1)}, u32[]{:S(2)}, u32[]{:S(2)}) collective-permute-start(bf16[8,96,256]{2,1,0:T(8,128)(2,1)S(1)} %copy-done.58), channel_id=1, source_target_pairs={{0,1},{1,0},{2,3},{3,2},{4,5},{5,4},{6,7},{7,6},{8,9},{9,8},{10,11... | collective-permute-start | bytes 1179656 | tf_op jit(solution)/shard_map/ppermute | solution.py:762
  441.3 41.5 %collective-permute-start.11 = (bf16[8,96,256]{2,1,0:T(8,128)(2,1)}, bf16[8,96,256]{2,1,0:T(8,128)(2,1)S(1)}, u32[]{:S(2)}, u32[]{:S(2)}) collective-permute-start(bf16[8,96,256]{2,1,0:T(8,128)(2,1)} %get-tuple-element.89), channel_id=1, source_target_pairs={{0,5},{1,4},{2,7},{3,6},{4,1},{5,0},{6,3},{7,2},{8,13},{9,12},{10,... | collective-permute-start | bytes 1179656 | tf_op jit(solution)/shard_map/ppermute | solution.py:762
  449.0 41.4 %collective-permute-start.12 = (bf16[8,96,256]{2,1,0:T(8,128)(2,1)}, bf16[8,96,256]{2,1,0:T(8,128)(2,1)}, u32[]{:S(2)}, u32[]{:S(2)}) collective-permute-start(bf16[8,96,256]{2,1,0:T(8,128)(2,1)} %get-tuple-element.90), channel_id=1, source_target_pairs={{0,6},{1,7},{2,4},{3,5},{4,2},{5,3},{6,0},{7,1},{8,14},{9,15},{10,... | collective-permute-start | bytes 1179656 | tf_op jit(solution)/shard_map/ppermute | solution.py:762
  456.6 42.4 %collective-permute-start.13 = (bf16[8,96,256]{2,1,0:T(8,128)(2,1)}, bf16[8,96,256]{2,1,0:T(8,128)(2,1)}, u32[]{:S(2)}, u32[]{:S(2)}) collective-permute-start(bf16[8,96,256]{2,1,0:T(8,128)(2,1)} %get-tuple-element.91), channel_id=1, source_target_pairs={{0,7},{1,6},{2,5},{3,4},{4,3},{5,2},{6,1},{7,0},{8,15},{9,14},{10,... | collective-permute-start | bytes 1179656 | tf_op jit(solution)/shard_map/ppermute | solution.py:762
  490.4 47.2 %collective-permute-start.51 = (bf16[8,96,256]{2,1,0:T(8,128)(2,1)}, bf16[8,96,256]{2,1,0:T(8,128)(2,1)S(1)}, u32[]{:S(2)}, u32[]{:S(2)}) collective-permute-start(bf16[8,96,256]{2,1,0:T(8,128)(2,1)} %get-tuple-element.135), channel_id=1, source_target_pairs={{0,3},{1,2},{2,1},{3,0},{4,7},{5,6},{6,5},{7,4},{8,11},{9,10},{10,... | collective-permute-start | bytes 1179656 | tf_op jit(solution)/shard_map/ppermute | solution.py:762
  (98 other events, 3498.4 us)
